TPU v7x, 8 devices: a whole 2x2x1 slice. The times are simulated.
8 devices in a mesh: dp: 2 (over z, y), tp: 4 (over x, core).
Axes of the slice: x: 2, y: 2, z: 1, core: 2. Of those that a mesh axis runs over, the one named last changes fastest.
Arguments:
- hidden: bfloat16 [512, 3072], P('dp'), parts along dimension 0
- positions: int32 [512], P('dp'), parts along dimension 0
- k_cache: bfloat16 [2, 512, 128, 8, 128], P(None, 'dp', None, 'tp'), parts along dimension 1
- v_cache: bfloat16 [2, 512, 128, 8, 128], P(None, 'dp', None, 'tp'), parts along dimension 1
- attn_norm: bfloat16 [2, 3072], replicated
- w_query: bfloat16 [2, 3072, 3072], P(None, None, 'tp')
- w_key: bfloat16 [2, 3072, 1024], P(None, None, 'tp')
- w_value: bfloat16 [2, 3072, 1024], P(None, None, 'tp')
- w_out: bfloat16 [2, 3072, 3072], P(None, 'tp')
- mlp_norm: bfloat16 [2, 3072], replicated
- w_gate: bfloat16 [2, 3072, 8192], P(None, None, 'tp')
- w_up: bfloat16 [2, 3072, 8192], P(None, None, 'tp')
- w_down: bfloat16 [2, 8192, 3072], P(None, 'tp')
Outputs:
- output 1: bfloat16 [512, 3072], P('dp'), parts along dimension 0
- output 2: bfloat16 [2, 512, 128, 8, 128], P(None, 'dp', None, 'tp'), parts along dimension 1
- output 3: bfloat16 [2, 512, 128, 8, 128], P(None, 'dp', None, 'tp'), parts along dimension 1
There are 2 independent parts. A program takes and returns all parts, laid end to end along the dimension named above; an argument that names none is the same for every part.
All inputs are finite; a program needn't handle non-finite values.
Results may differ from a plain program's by a relative error of at most 0.02.
Values are sent between devices in bfloat16 or wider.
A program may use at most 1 GiB of HBM per device.

v0:
```python
import math
import jax
import jax.numpy as jnp
from jax import lax
from jax.sharding import PartitionSpec as P


def rms_norm(hidden, weight):
    hidden_f32 = hidden.astype(jnp.float32)
    mean_sq = jnp.mean(hidden_f32 * hidden_f32, axis=-1, keepdims=True)
    return (hidden_f32 * lax.rsqrt(mean_sq + 1e-5) * weight.astype(jnp.float32)).astype(jnp.bfloat16)


def rope_tables(positions, head_dim):
    half_dim = head_dim // 2
    inv_freq = jnp.power(500000.0, -jnp.arange(half_dim, dtype=jnp.float32) * (2.0 / head_dim))
    wavelen = (2.0 * math.pi) / inv_freq
    smooth = (8192.0 / wavelen - 1.0) / 3.0
    blended = (1.0 - smooth) * inv_freq / 8.0 + smooth * inv_freq
    scaled = jnp.where(wavelen < 2048.0, inv_freq, jnp.where(wavelen > 8192.0, inv_freq / 8.0, blended))
    angles = positions.astype(jnp.float32)[:, None] * scaled[None, :]
    return jnp.cos(angles), jnp.sin(angles)


def apply_rope(vectors, cos_tab, sin_tab):
    half_dim = vectors.shape[-1] // 2
    vec_f32 = vectors.astype(jnp.float32)
    first = vec_f32[..., :half_dim]
    second = vec_f32[..., half_dim:]
    cos_b = cos_tab[:, None, :]
    sin_b = sin_tab[:, None, :]
    return jnp.concatenate([first * cos_b - second * sin_b, second * cos_b + first * sin_b], axis=-1).astype(jnp.bfloat16)


def attend_split(query, k_old, v_old, key_new, value_new, before):
    score_scale = query.shape[-1] ** -0.5
    scores = jnp.einsum('bkgd,bskd->bkgs', query, k_old, preferred_element_type=jnp.float32) * score_scale
    scores = jnp.where(before, scores, -jnp.inf)
    score_new = jnp.einsum('clhe,cle->clh', query, key_new, preferred_element_type=jnp.float32) * score_scale
    row_peak = jnp.maximum(jnp.max(scores, axis=-1), score_new)
    weight_old = jnp.exp(scores - row_peak[..., None])
    weight_new = jnp.exp(score_new - row_peak)
    inv_total = 1.0 / (jnp.sum(weight_old, axis=-1) + weight_new)
    prob_old = (weight_old * inv_total[..., None]).astype(jnp.bfloat16)
    prob_new = (weight_new * inv_total).astype(jnp.bfloat16)
    attn_out = jnp.einsum('bkgs,bskd->bkgd', prob_old, v_old, preferred_element_type=jnp.float32)
    attn_out = attn_out + prob_new[..., None].astype(jnp.float32) * value_new[:, :, None, :].astype(jnp.float32)
    return attn_out.astype(jnp.bfloat16)


def attention_block(hidden, norm_weight, wq_layer, wk_layer, wv_layer, wo_layer, k_old, v_old, cos_tab, sin_tab, before):
    batch_size = hidden.shape[0]
    kv_heads = k_old.shape[2]
    head_dim = k_old.shape[3]
    q_heads = wq_layer.shape[1] // head_dim
    normed = rms_norm(hidden, norm_weight)
    query = jnp.dot(normed, wq_layer, preferred_element_type=jnp.float32).astype(jnp.bfloat16)
    key_new = jnp.dot(normed, wk_layer, preferred_element_type=jnp.float32).astype(jnp.bfloat16)
    value_new = jnp.dot(normed, wv_layer, preferred_element_type=jnp.float32).astype(jnp.bfloat16)
    query = apply_rope(query.reshape(batch_size, q_heads, head_dim), cos_tab, sin_tab)
    key_new = apply_rope(key_new.reshape(batch_size, kv_heads, head_dim), cos_tab, sin_tab)
    value_new = value_new.reshape(batch_size, kv_heads, head_dim)
    attended = attend_split(query.reshape(batch_size, kv_heads, q_heads // kv_heads, head_dim), k_old, v_old, key_new, value_new, before)
    mixed = jnp.dot(attended.reshape(batch_size, q_heads * head_dim), wo_layer, preferred_element_type=jnp.float32)
    return mixed.astype(jnp.bfloat16), key_new, value_new


def mlp_block(hidden, norm_weight, wg_layer, wu_layer, wd_layer):
    normed = rms_norm(hidden, norm_weight)
    gate_proj = jnp.dot(normed, wg_layer, preferred_element_type=jnp.float32).astype(jnp.bfloat16)
    up_proj = jnp.dot(normed, wu_layer, preferred_element_type=jnp.float32).astype(jnp.bfloat16)
    activated = (jax.nn.silu(gate_proj.astype(jnp.float32)) * up_proj.astype(jnp.float32)).astype(jnp.bfloat16)
    return jnp.dot(activated, wd_layer, preferred_element_type=jnp.float32).astype(jnp.bfloat16)


def write_rows(cache, rows, positions):
    at_pos = (jnp.arange(cache.shape[2])[None, :] == positions[:, None])[None, :, :, None, None]
    return jnp.where(at_pos, rows[:, :, None], cache)


def solution(mesh):
    row_spec = P('dp', None)
    pos_spec = P('dp')
    cache_spec = P(None, 'dp', None, 'tp', None)
    norm_spec = P(None, None)
    col_spec = P(None, None, 'tp')
    split_rows = P(None, 'tp', None)

    def local_step(hidden, positions, k_cache, v_cache, attn_norm, w_query, w_key, w_value, w_out, mlp_norm, w_gate, w_up, w_down):
        cos_tab, sin_tab = rope_tables(positions, k_cache.shape[4])
        before = (jnp.arange(k_cache.shape[2])[None, :] < positions[:, None])[:, None, None, :]
        k_rows = []
        v_rows = []
        for layer in range(k_cache.shape[0]):
            part_out, key_new, value_new = attention_block(hidden, attn_norm[layer], w_query[layer], w_key[layer], w_value[layer], w_out[layer], k_cache[layer], v_cache[layer], cos_tab, sin_tab, before)
            hidden = hidden + lax.psum(part_out, 'tp')
            part_out = mlp_block(hidden, mlp_norm[layer], w_gate[layer], w_up[layer], w_down[layer])
            hidden = hidden + lax.psum(part_out, 'tp')
            k_rows.append(key_new)
            v_rows.append(value_new)
        k_out = write_rows(k_cache, jnp.stack(k_rows), positions)
        v_out = write_rows(v_cache, jnp.stack(v_rows), positions)
        return hidden, k_out, v_out

    return jax.shard_map(local_step, mesh=mesh, in_specs=(row_spec, pos_spec, cache_spec, cache_spec, norm_spec, col_spec, col_spec, col_spec, split_rows, norm_spec, col_spec, col_spec, split_rows), out_specs=(row_spec, cache_spec, cache_spec), check_vma=False)
```

profile of v0, /device:TPU:0, one launch (start us, length us, event | category | flops | bytes accessed | tf_op | source)
XLA Modules:
  0.0 417.3 jit_solution(4408820072380232459)
XLA Ops:
  7.2 0.7 convert_element_type.192
  7.9 1.4 iota_compare_fusion
  9.3 1.9 fusion.46
  11.3 1.4 slice_convert_fusion.1
  12.7 2.8 fusion.127
  15.5 1.0 fusion.124
  16.5 0.3 multiply_cosine_fusion
  16.9 0.1 copy.106
  17.1 0.1 copy.74
  17.2 0.3 copy-done.4
  17.5 4.7 %fusion.115 = f32[256,768]{1,0:T(8,128)} fusion(bf16[2,3072,768]{2,1,0:T(8,128)(2,1)} %param.18, bf16[256,3072]{1,0:T(8,128)(2,1)S(1)} %copy-done, f32[3072]{0:T(1024)S(1)} %bitcast.179, f32[256]{0:T(256)S(1)} %add_rsqrt_fusion.3), kind=kOutput, calls=%fused_computation.103 | convolution fusion | flops 1211498496 | bytes 7091200 | tf_op jit(solution)/shard_map/dot_general | solution.py:57
  22.2 1.4 copy.64
  23.7 0.3 copy.66
  24.0 0.3 copy.65
  24.4 1.5 multiply_reduce_fusion.1
  25.9 0.1 copy.95
  26.0 28.0 %fusion.164 = (bf16[1,256,128,2,128]{4,3,2,1,0:T(2,128)(2,1)}, bf16[1,256,128,2,128]{4,3,2,1,0:T(2,128)(2,1)}) fusion(bf16[2,256,128,2,128]{4,3,2,1,0:T(2,128)(2,1)} %param.15), kind=kLoop, calls=%fused_computation.164 | loop fusion | bytes 67108864 | tf_op jit(solution)/shard_map/slice | solution.py:95
  54.1 13.5 %fusion.166 = (f32[256,2,3]{2,1,0:T(2,128)S(1)}, f32[256,2,3,128]{3,2,1,0:T(4,128)}) fusion(bf16[1,256,128,2,128]{4,3,2,1,0:T(2,128)(2,1)} %get-tuple-element.14, bf16[256,2,3,64]{3,2,1,0:T(4,128)(2,1)S(1)} %copy.66, bf16[256,2,3,64]{3,2,1,0:T(4,128)(2,1)S(1)} %copy.65, pred[256,128]{1,0:T(8,128)(4,1)S(1)} %copy-done.15), kind=kOutput, calls=%fused_computation.166 | convolution fusion | flops 51706368 | bytes 17995776 | tf_op jit(solution)/shard_map/bkgd,bskd->bkgs/dot_general | solution.py:37
  67.6 0.1 copy.68
  67.7 0.2 copy.69
  67.9 2.5 fusion.138
  70.4 0.1 copy.70
  70.5 0.2 copy.73
  70.7 0.9 copy.71
  71.6 26.0 %fusion.165 = (bf16[1,256,128,2,128]{4,3,2,1,0:T(2,128)(2,1)}, bf16[1,256,128,2,128]{4,3,2,1,0:T(2,128)(2,1)S(1)}) fusion(bf16[2,256,128,2,128]{4,3,2,1,0:T(2,128)(2,1)} %param.16), kind=kLoop, calls=%fused_computation.165 | loop fusion | bytes 67108864 | tf_op jit(solution)/shard_map/slice | solution.py:95
  97.6 5.8 %fusion.111 = bf16[256,2,3,128]{3,2,1,0:T(4,128)(2,1)} fusion(bf16[1,256,128,2,128]{4,3,2,1,0:T(2,128)(2,1)S(1)} %get-tuple-element.16, f32[256,2,3,128]{3,2,1,0:T(4,128)S(1)} %copy-done.3, f32[256,2,128]{2,1,0:T(2,128)S(1)} %copy.74, f32[256,2,3]{2,1,0:T(2,128)S(1)} %copy.73, f32[256,2,3]{2,1,0:T(2,128)S(1)} %copy-done.12, f32[256,2,3]{2,1,0:T(2,128)S(1)} %copy.69), kind=kOutput, calls=%fused_computation.101 | convolution fusion | flops 51511296 | bytes 18237440 | tf_op jit(solution)/shard_map/bkgs,bskd->bkgd/dot_general | solution.py:46
  103.4 1.3 copy.75
  104.7 4.9 %fusion.34 = bf16[256,3072]{1,0:T(8,128)(2,1)} fusion(bf16[256,768]{0,1:T(8,128)(2,1)S(1)} %bitcast.168, bf16[2,768,3072]{2,1,0:T(8,128)(2,1)} %param.21), kind=kOutput, calls=%fused_computation.48 | convolution fusion | flops 1208745984 | bytes 6684672 | tf_op jit(solution)/shard_map/dot_general | solution.py:64
  109.6 0.2 all-reduce.7.cloned.1.call-start
  109.8 0.6 slice_convert_fusion
  110.4 39.5 %all-reduce.5.cloned.1.call-done = bf16[256,3072]{1,0:T(8,128)(2,1)} async-done(((bf16[256,3072]{1,0:T(8,128)(2,1)}), bf16[256,3072]{1,0:T(8,128)(2,1)}) %all-reduce.5.cloned.1.call-update) | async-done | bytes 1572880 | tf_op jit(solution)/shard_map/psum | solution.py:96
  149.9 2.1 fusion.49
  152.1 8.0 %fusion.58 = bf16[256,2048]{1,0:T(8,128)(2,1)S(1)} fusion(bf16[2,3072,2048]{2,1,0:T(8,128)(2,1)} %param.23, bf16[256,3072]{1,0:T(8,128)(2,1)S(1)} %get-tuple-element.10, f32[3072]{0:T(1024)S(1)} %bitcast.180, f32[256]{0:T(256)S(1)} %add_rsqrt_fusion.2), kind=kOutput, calls=%fused_computation.68 | convolution fusion | flops 3224895488 | bytes 15217664 | tf_op jit(solution)/shard_map/dot_general | solution.py:70
  160.1 16.2 %fusion.40 = bf16[256,3072]{1,0:T(8,128)(2,1)} fusion(bf16[2,2048,3072]{2,1,0:T(8,128)(2,1)} %param.25, bf16[2,3072,2048]{2,1,0:T(8,128)(2,1)} %param.24, bf16[256,2048]{1,0:T(8,128)(2,1)S(1)} %fusion.58, bf16[256,3072]{1,0:T(8,128)(2,1)S(1)} %get-tuple-element.10, f32[3072]{0:T(1024)S(1)} %bitcast.181, f32[256]{0:T(256)S(1)} %add_rsqrt_fusion.2), kind=kOutput, calls=%fused_computation.50 | convolution fusion | flops 6451101696 | bytes 29373440 | tf_op jit(solution)/shard_map/dot_general | solution.py:73
  176.4 37.4 %all-reduce.7.cloned.1.call-done = bf16[256,3072]{1,0:T(8,128)(2,1)} async-done(((bf16[256,3072]{1,0:T(8,128)(2,1)}), bf16[256,3072]{1,0:T(8,128)(2,1)}) %all-reduce.7.cloned.1.call-update) | async-done | bytes 1572880 | tf_op jit(solution)/shard_map/psum | solution.py:98
  213.8 2.3 fusion.52
  216.1 0.9 fusion.133
  217.1 0.9 copy-done.21
  218.0 1.0 fusion.130
  218.9 4.7 %fusion.121 = f32[256,768]{1,0:T(8,128)} fusion(bf16[2,3072,768]{2,1,0:T(8,128)(2,1)} %param.18, bf16[256,3072]{1,0:T(8,128)(2,1)S(1)} %get-tuple-element.8, f32[3072]{0:T(1024)S(1)} %bitcast.176, f32[256]{0:T(256)S(1)} %add_rsqrt_fusion.1), kind=kOutput, calls=%fused_computation.105 | convolution fusion | flops 1211498496 | bytes 7091200 | tf_op jit(solution)/shard_map/dot_general | solution.py:57
  223.7 0.1 copy.107
  223.9 0.8 copy.86
  224.7 1.4 copy.76
  226.2 0.3 copy.78
  226.5 0.3 copy.77
  226.9 13.7 %fusion.167 = (f32[256,2,3]{2,1,0:T(2,128)S(1)}, f32[256,2,3,128]{3,2,1,0:T(4,128)}) fusion(bf16[1,256,128,2,128]{4,3,2,1,0:T(2,128)(2,1)} %get-tuple-element.13, bf16[256,2,3,64]{3,2,1,0:T(4,128)(2,1)S(1)} %copy.78, bf16[256,2,3,64]{3,2,1,0:T(4,128)(2,1)S(1)} %copy.77, pred[256,128]{1,0:T(8,128)(4,1)S(1)} %copy-done.16), kind=kOutput, calls=%fused_computation.167 | convolution fusion | flops 51706368 | bytes 17995776 | tf_op jit(solution)/shard_map/bkgd,bskd->bkgs/dot_general | solution.py:37
  240.6 1.5 multiply_reduce_fusion
  242.1 0.1 copy.101
  242.3 0.1 copy.80
  242.4 0.2 copy.81
  242.6 2.5 fusion.139
  245.2 0.9 copy.85
  246.1 0.9 copy.83
  247.0 11.3 %fusion.110 = bf16[256,2,3,128]{3,2,1,0:T(4,128)(2,1)S(1)} fusion(bf16[1,256,128,2,128]{4,3,2,1,0:T(2,128)(2,1)} %get-tuple-element.15, f32[256,2,3,128]{3,2,1,0:T(4,128)S(1)} %copy-done.2, f32[256,2,128]{2,1,0:T(2,128)} %copy.86, f32[256,2,3]{2,1,0:T(2,128)} %copy.85, f32[256,2,3]{2,1,0:T(2,128)} %copy.83, f32[256,2,3]{2,1,0:T(2,128)S(1)} %copy.81), kind=kOutput, calls=%fused_computation.100 | convolution fusion | flops 51511296 | bytes 18237440 | tf_op jit(solution)/shard_map/bkgs,bskd->bkgd/dot_general | solution.py:46
  258.3 0.3 copy.87
  258.6 5.0 %fusion.37 = bf16[256,3072]{1,0:T(8,128)(2,1)} fusion(bf16[256,768]{0,1:T(8,128)(2,1)S(1)} %bitcast.169, bf16[2,768,3072]{2,1,0:T(8,128)(2,1)} %param.21), kind=kOutput, calls=%fused_computation.49 | convolution fusion | flops 1208745984 | bytes 6684672 | tf_op jit(solution)/shard_map/dot_general | solution.py:64
  263.7 0.2 copy.89
  263.9 0.9 copy.88
  264.8 36.3 %all-reduce.9.cloned.1.call-done = bf16[256,3072]{1,0:T(8,128)(2,1)} async-done(((bf16[256,3072]{1,0:T(8,128)(2,1)}), bf16[256,3072]{1,0:T(8,128)(2,1)}) %all-reduce.9.cloned.1.call-update) | async-done | bytes 1572880 | tf_op jit(solution)/shard_map/psum | solution.py:96
  301.1 2.1 fusion.55
  303.2 8.0 %fusion.73 = bf16[256,2048]{1,0:T(8,128)(2,1)S(1)} fusion(bf16[2,3072,2048]{2,1,0:T(8,128)(2,1)} %param.23, bf16[256,3072]{1,0:T(8,128)(2,1)S(1)} %get-tuple-element.4, f32[3072]{0:T(1024)S(1)} %bitcast.172, f32[256]{0:T(256)S(1)} %add_rsqrt_fusion), kind=kOutput, calls=%fused_computation.73 | convolution fusion | flops 3224895488 | bytes 15217664 | tf_op jit(solution)/shard_map/dot_general | solution.py:70
  311.3 16.2 %fusion.43 = bf16[256,3072]{1,0:T(8,128)(2,1)} fusion(bf16[2,2048,3072]{2,1,0:T(8,128)(2,1)} %param.25, bf16[2,3072,2048]{2,1,0:T(8,128)(2,1)} %param.24, bf16[256,2048]{1,0:T(8,128)(2,1)S(1)} %fusion.73, bf16[256,3072]{1,0:T(8,128)(2,1)S(1)} %get-tuple-element.4, f32[3072]{0:T(1024)S(1)} %bitcast.173, f32[256]{0:T(256)S(1)} %add_rsqrt_fusion), kind=kOutput, calls=%fused_computation.51 | convolution fusion | flops 6451101696 | bytes 29373440 | tf_op jit(solution)/shard_map/dot_general | solution.py:73
  327.6 79.6 %broadcast_select_fusion = (bf16[2,256,128,2,128]{4,3,2,1,0:T(2,128)(2,1)}, bf16[2,256,128,2,128]{4,3,2,1,0:T(2,128)(2,1)}) fusion(bf16[2,256,128,2,128]{4,3,2,1,0:T(2,128)(2,1)} %param.16, pred[256,128]{1,0:T(8,128)(4,1)S(1)} %copy-done.13, bf16[2,256,2,128]{3,2,1,0:T(2,128)(2,1)S(1)} %copy.89, bf16[2,256,128,2,128]{4,3,2,1,0:T(2,128)(2,1)} %param.15, ...), kind=kLoop, calls=%fused_computation | loop fusion | flops 33554432 | bytes 134774784 | tf_op jit(solution)/shard_map/jit(_where)/select_n | solution.py:78
  407.2 3.1 add.113
  (70 shorter events, 1.0 us)
Async XLA Ops:
  7.2 142.7 %all-reduce.5.cloned.1.call-start = ((), (), s32[]{:S(2)}) async-start(), calls=%async_computation | async-start | bytes 3145728 | tf_op jit(solution)/shard_map/psum | solution.py:96
  9.3 6.2 %copy-start = (bf16[256,3072]{1,0:T(8,128)(2,1)S(1)}, bf16[256,3072]{1,0:T(8,128)(2,1)}, u32[]{:S(2)}) copy-start(bf16[256,3072]{1,0:T(8,128)(2,1)} %param.13) | copy-start | bytes 4718596
  9.3 6.2 %copy-start.20 = (bf16[2,3072,256]{2,1,0:T(8,128)(2,1)S(1)}, bf16[2,3072,256]{2,1,0:T(8,128)(2,1)}, u32[]{:S(2)}) copy-start(bf16[2,3072,256]{2,1,0:T(8,128)(2,1)} %param.19) | copy-start | bytes 9437188
  15.5 1.6 copy-start.8
  16.9 0.6 copy-start.4
  16.9 0.7 copy-start.6
  26.0 28.0 %copy-start.15 = (pred[256,128]{1,0:T(8,128)(4,1)S(1)}, pred[256,128]{1,0:T(8,128)(4,1)}, u32[]{:S(2)}) copy-start(pred[256,128]{1,0:T(8,128)(4,1)} %get-tuple-element.34) | copy-start | bytes 98308
  71.6 26.0 %copy-start.3 = (f32[256,2,3,128]{3,2,1,0:T(4,128)S(1)}, f32[256,2,3,128]{3,2,1,0:T(4,128)}, u32[]{:S(2)}) copy-start(f32[256,2,3,128]{3,2,1,0:T(4,128)} %get-tuple-element.36) | copy-start | bytes 2359300
  71.6 26.0 %copy-start.12 = (f32[256,2,3]{2,1,0:T(2,128)S(1)}, f32[256,2,3]{2,1,0:T(2,128)}, u32[]{:S(2)}) copy-start(f32[256,2,3]{2,1,0:T(2,128)} %copy.71) | copy-start | bytes 18436
  104.7 5.2 %copy-start.14 = (bf16[2,3072]{1,0:T(2,128)(2,1)S(1)}, bf16[2,3072]{1,0:T(2,128)(2,1)}, u32[]{:S(2)}) copy-start(bf16[2,3072]{1,0:T(2,128)(2,1)} %param.22) | copy-start | bytes 36868
  109.6 104.2 %all-reduce.7.cloned.1.call-start = ((), (), s32[]{:S(2)}) async-start(), calls=%async_computation.1 | async-start | bytes 3145728 | tf_op jit(solution)/shard_map/psum | solution.py:98
  176.3 39.8 %copy-start.18 = (f32[1,3072]{1,0:T(1,128)S(1)}, f32[1,3072]{1,0:T(1,128)}, u32[]{:S(2)}) copy-start(f32[1,3072]{1,0:T(1,128)} %get-tuple-element.29) | copy-start | bytes 36868
  176.3 124.7 %all-reduce.9.cloned.1.call-start = ((), (), s32[]{:S(2)}) async-start(), calls=%async_computation.2 | async-start | bytes 3145728 | tf_op jit(solution)/shard_map/psum | solution.py:96
  213.8 2.4 copy-start.19
  216.1 1.9 copy-start.21
  218.0 5.9 %copy-start.10 = (bf16[256,256]{0,1:T(8,128)(2,1)}, bf16[256,256]{0,1:T(8,128)(2,1)S(1)}, u32[]{:S(2)}) copy-start(bf16[256,256]{0,1:T(8,128)(2,1)S(1)} %fusion.133) | copy-start | bytes 393220
  223.6 3.2 copy-start.16
  242.1 4.8 %copy-start.2 = (f32[256,2,3,128]{3,2,1,0:T(4,128)S(1)}, f32[256,2,3,128]{3,2,1,0:T(4,128)}, u32[]{:S(2)}) copy-start(f32[256,2,3,128]{3,2,1,0:T(4,128)} %get-tuple-element.38) | copy-start | bytes 2359300
  258.6 5.1 %copy-start.9 = (bf16[256,256]{0,1:T(8,128)(2,1)S(1)}, bf16[256,256]{0,1:T(8,128)(2,1)}, u32[]{:S(2)}) copy-start(bf16[256,256]{0,1:T(8,128)(2,1)} %copy-done.8) | copy-start | bytes 393220
  258.6 5.1 %copy-start.11 = (bf16[256,256]{0,1:T(8,128)(2,1)S(1)}, bf16[256,256]{0,1:T(8,128)(2,1)}, u32[]{:S(2)}) copy-start(bf16[256,256]{0,1:T(8,128)(2,1)} %copy-done.10) | copy-start | bytes 393220
  258.6 5.3 %copy-start.5 = (bf16[256,2,64]{0,2,1:T(8,128)(2,1)S(1)}, bf16[256,2,64]{0,2,1:T(8,128)(2,1)}, u32[]{:S(2)}) copy-start(bf16[256,2,64]{0,2,1:T(8,128)(2,1)} %copy-done.4) | copy-start | bytes 196612
  258.6 5.3 %copy-start.7 = (bf16[256,2,64]{0,2,1:T(8,128)(2,1)S(1)}, bf16[256,2,64]{0,2,1:T(8,128)(2,1)}, u32[]{:S(2)}) copy-start(bf16[256,2,64]{0,2,1:T(8,128)(2,1)} %copy-done.6) | copy-start | bytes 196612
  263.6 143.6 %all-reduce.11.cloned.1.call-start = ((), (), s32[]{:S(2)}) async-start(), calls=%async_computation.3 | async-start | bytes 3145728 | tf_op jit(solution)/shard_map/psum | solution.py:98
  263.7 39.5 %copy-start.17 = (f32[1,3072]{1,0:T(1,128)S(1)}, f32[1,3072]{1,0:T(1,128)}, u32[]{:S(2)}) copy-start(f32[1,3072]{1,0:T(1,128)} %get-tuple-element.27) | copy-start | bytes 36868
  311.3 16.3 %copy-start.1 = (bf16[2,256,2,128]{3,2,1,0:T(2,128)(2,1)S(1)}, bf16[2,256,2,128]{3,2,1,0:T(2,128)(2,1)}, u32[]{:S(2)}) copy-start(bf16[2,256,2,128]{3,2,1,0:T(2,128)(2,1)} %copy.88) | copy-start | bytes 786436
  311.3 16.3 %copy-start.13 = (pred[256,128]{1,0:T(8,128)(4,1)S(1)}, pred[256,128]{1,0:T(8,128)(4,1)}, u32[]{:S(2)}) copy-start(pred[256,128]{1,0:T(8,128)(4,1)} %get-tuple-element.33) | copy-start | bytes 98308
Sparse Core Ops, SparseCore 0:
  109.7 40.1 all-reduce.4
  176.5 37.2 all-reduce.6
  263.7 37.3 all-reduce.8
  327.7 37.3 all-reduce.10
where the time goes:
time: 423 us; the launch traced here: 417 us
  matrix products  118 us (28%)
  waiting for transfers between devices  113 us (27%)
  other arithmetic  104 us (25%)
  local copies, waits for them, and re-layouts  67.1 us (16%)
  between operations  14.8 us (3%)
    psum x4, waiting for transfers between devices, local_step(): hidden = hidden + lax.psum(part_out, 'tp')  113 us
    select_n x1, other arithmetic, write_rows(): return jnp.where(at_pos, rows[:, :, None], cache)  79.6 us
    dot_general x2, matrix products, mlp_block(): jnp.dot(activated, wd_layer, preferred_element_type=jnp.float32)  32.4 us
    slice x1, local copies, waits for them, and re-layouts, local_step(): k_cache[layer]  28 us
    dot_general x2, matrix products, attend_split(): jnp.einsum('bkgd,bskd->bkgs', query, k_old, preferred_element_type=jnp.fl...  27.3 us
    slice x1, local copies, waits for them, and re-layouts, local_step(): v_cache[layer]  26 us
    dot_general x2, matrix products, attend_split(): jnp.einsum('bkgs,bskd->bkgd', prob_old, v_old, preferred_element_type=jnp...  17.1 us
    dot_general x2, matrix products, mlp_block(): jnp.dot(normed, wg_layer, preferred_element_type=jnp.float32)  16.1 us
  transfers between devices with their start and end apart: 4, of which 3 were waited for; matrix products, arithmetic and copies ran while one was open for 19% of the time, Pallas kernels for 0%

commit v1 on v0

v1 whole, which is shorter than its diff:
```python
import functools
import math
import jax
import jax.numpy as jnp
from jax import lax
from jax.experimental import pallas as pl
from jax.experimental.pallas import tpu as pltpu
from jax.sharding import PartitionSpec as P

BF = jnp.bfloat16
F32 = jnp.float32
MESH = pl.DeviceIdType.MESH
EPS = 1e-5
NEG = -1e30


def rope_full(positions, head_dim):
    half_dim = head_dim // 2
    inv_freq = jnp.power(500000.0, -jnp.arange(half_dim, dtype=F32) * (2.0 / head_dim))
    wavelen = (2.0 * math.pi) / inv_freq
    smooth = (8192.0 / wavelen - 1.0) / 3.0
    blended = (1.0 - smooth) * inv_freq / 8.0 + smooth * inv_freq
    scaled = jnp.where(wavelen < 2048.0, inv_freq, jnp.where(wavelen > 8192.0, inv_freq / 8.0, blended))
    angles = positions.astype(F32)[:, None] * scaled[None, :]
    cos, sin = jnp.cos(angles), jnp.sin(angles)
    return jnp.concatenate([cos, cos], axis=-1), jnp.concatenate([-sin, sin], axis=-1)


def normed(x_f32, weight_f32):
    mean_sq = jnp.mean(x_f32 * x_f32, axis=-1, keepdims=True)
    return (x_f32 * lax.rsqrt(mean_sq + EPS) * weight_f32).astype(BF)


BLK = 16
DEPTH = 8
LAG = 3


def attn_kernel(layer, aliased, pos_ref, x_ref, norm_ref, cos_ref, sin_ref, wq_hbm, wk_hbm, wv_hbm, k_hbm, v_hbm, *rest):
    if aliased:
        rest = rest[2:]
    o_ref, ko_hbm, vo_hbm, w_buf, h_buf, qkv, q_rows, k_rows, v_rows, kbuf, vbuf, wsem, insem, outsem = rest
    batch = x_ref.shape[0]
    nblk = batch // BLK
    qcols = wq_hbm.shape[2]
    kcols = wk_hbm.shape[2]
    heads = qcols // 128

    w_copies = [
        pltpu.make_async_copy(wq_hbm.at[layer], w_buf.at[:, pl.ds(0, qcols)], wsem.at[0]),
        pltpu.make_async_copy(wk_hbm.at[layer], w_buf.at[:, pl.ds(qcols, kcols)], wsem.at[1]),
        pltpu.make_async_copy(wv_hbm.at[layer], w_buf.at[:, pl.ds(qcols + kcols, kcols)], wsem.at[2]),
    ]
    for c in w_copies:
        c.start()

    def in_copies(i):
        slot = lax.rem(i, DEPTH)
        rows = pl.ds(i * BLK, BLK)
        return (pltpu.make_async_copy(k_hbm.at[layer, rows], kbuf.at[slot], insem.at[0, slot]),
                pltpu.make_async_copy(v_hbm.at[layer, rows], vbuf.at[slot], insem.at[1, slot]))

    def out_copies(i):
        slot = lax.rem(i, DEPTH)
        rows = pl.ds(i * BLK, BLK)
        return (pltpu.make_async_copy(kbuf.at[slot], ko_hbm.at[layer, rows], outsem.at[0, slot]),
                pltpu.make_async_copy(vbuf.at[slot], vo_hbm.at[layer, rows], outsem.at[1, slot]))

    for i in range(DEPTH - LAG):
        for c in in_copies(i):
            c.start()

    h_buf[...] = normed(x_ref[...].astype(F32), norm_ref[layer:layer + 1, :].astype(F32))
    for c in w_copies:
        c.wait()

    @pl.loop(0, (qcols + 2 * kcols) // 256)
    def _(n):
        cols = pl.ds(pl.multiple_of(n * 256, 256), 256)
        qkv[n] = jnp.dot(h_buf[...], w_buf[:, cols], preferred_element_type=F32).astype(BF).astype(F32)

    cos_b = cos_ref[...]
    sin_b = sin_ref[...]

    def rope(vec):
        return (vec * cos_b + pltpu.roll(vec, 64, 1) * sin_b).astype(BF).astype(F32)

    zero = jnp.zeros((batch, 128), F32)
    for j in range(8):
        vec = rope(qkv[j // 2][:, (j % 2) * 128:(j % 2) * 128 + 128]) if j < heads else zero
        q_rows[pl.ds(j, batch, stride=8), :] = vec
    for h in range(2):
        k_vec = rope(qkv[heads // 2][:, h * 128:h * 128 + 128])
        v_vec = qkv[heads // 2 + 1][:, h * 128:h * 128 + 128]
        for r in range(4):
            k_rows[pl.ds(2 * r + h, batch, stride=8), :] = k_vec
            v_rows[pl.ds(2 * r + h, batch, stride=8), :] = v_vec

    col = lax.broadcasted_iota(jnp.int32, (8, 256), 1)
    row = lax.broadcasted_iota(jnp.int32, (8, 256), 0)
    own = (col & 1) == jnp.where(row >= heads // 2, 1, 0)
    key_row = jnp.where(own, col >> 1, 4096)
    seq_in_group = lax.broadcasted_iota(jnp.int32, (16, 128), 0) >> 1
    scale = 128 ** -0.5

    @pl.loop(0, nblk)
    def _(i):
        slot = lax.rem(i, DEPTH)
        for c in in_copies(i):
            c.wait()
        for b in range(BLK):
            pos = pos_ref[i * BLK + b]
            group = pl.ds(pl.multiple_of((pos >> 3) * 16, 16), 16)
            hit = seq_in_group == (pos & 7)
            rows = pl.ds(pl.multiple_of((i * BLK + b) * 8, 8), 8)
            for buf, new in ((kbuf, k_rows), (vbuf, v_rows)):
                new8 = new[rows, :]
                new16 = jnp.concatenate([new8, new8], axis=0)
                old16 = buf[slot, b, group, :].astype(F32)
                buf[slot, b, group, :] = jnp.where(hit, new16, old16).astype(BF)
        zero8 = jnp.zeros((8, 128), F32)
        for p in range(BLK // 2):
            first = i * BLK + 2 * p
            qa = q_rows[pl.ds(pl.multiple_of(first * 8, 8), 8), :]
            qb = q_rows[pl.ds(pl.multiple_of(first * 8 + 8, 8), 8), :]
            q2 = jnp.concatenate([jnp.concatenate([qa, zero8], axis=1), jnp.concatenate([zero8, qb], axis=1)], axis=0).astype(BF)
            k2 = jnp.concatenate([kbuf[slot, 2 * p], kbuf[slot, 2 * p + 1]], axis=1)
            v2 = jnp.concatenate([vbuf[slot, 2 * p], vbuf[slot, 2 * p + 1]], axis=1)
            s = lax.dot_general(q2, k2, (((1,), (1,)), ((), ())), preferred_element_type=F32) * scale
            keep = jnp.concatenate([key_row <= pos_ref[first], key_row <= pos_ref[first + 1]], axis=0)
            s = jnp.where(keep, s, NEG)
            e = jnp.exp(s - jnp.max(s, axis=-1, keepdims=True))
            w = (e * (1.0 / jnp.sum(e, axis=-1, keepdims=True))).astype(BF)
            o = jnp.dot(w, v2, preferred_element_type=F32)
            o_ref[pl.ds(pl.multiple_of(first * 8, 8), 8), :] = o[0:8, 0:128]
            o_ref[pl.ds(pl.multiple_of(first * 8 + 8, 8), 8), :] = o[8:16, 128:256]
        for c in out_copies(i):
            c.start()

        @pl.when(i >= LAG)
        def _():
            for c in out_copies(i - LAG):
                c.wait()

        @pl.when(i + DEPTH - LAG < nblk)
        def _():
            for c in in_copies(i + DEPTH - LAG):
                c.start()

    for i in range(nblk - LAG, nblk):
        for c in out_copies(i):
            c.wait()


def attention(layer, positions, hidden, norm, cos_f, sin_f, wq, wk, wv, k_cache, v_cache, prev):
    batch = hidden.shape[0]
    dim = hidden.shape[1]
    cols = wq.shape[2] + 2 * wk.shape[2]
    anyspec = pl.BlockSpec(memory_space=pl.ANY)
    vmem = pl.BlockSpec(memory_space=pltpu.VMEM)
    args = [positions, hidden, norm, cos_f, sin_f, wq, wk, wv, k_cache, v_cache]
    in_specs = [pl.BlockSpec(memory_space=pltpu.SMEM), vmem, vmem, vmem, vmem] + [anyspec] * 5
    aliases = {}
    if prev is not None:
        args += list(prev)
        in_specs += [anyspec] * 2
        aliases = {10: 1, 11: 2}
    return pl.pallas_call(
        functools.partial(attn_kernel, layer, prev is not None),
        out_shape=(jax.ShapeDtypeStruct((batch * 8, 128), F32),
                   jax.ShapeDtypeStruct(k_cache.shape, BF), jax.ShapeDtypeStruct(v_cache.shape, BF)),
        in_specs=in_specs,
        out_specs=(vmem, anyspec, anyspec),
        scratch_shapes=[
            pltpu.VMEM((dim, cols), BF),
            pltpu.VMEM((batch, dim), BF),
            pltpu.VMEM((cols // 256, batch, 256), F32),
            pltpu.VMEM((batch * 8, 128), F32),
            pltpu.VMEM((batch * 8, 128), F32),
            pltpu.VMEM((batch * 8, 128), F32),
            pltpu.VMEM((DEPTH, BLK, 256, 128), BF),
            pltpu.VMEM((DEPTH, BLK, 256, 128), BF),
            pltpu.SemaphoreType.DMA((3,)),
            pltpu.SemaphoreType.DMA((2, DEPTH)),
            pltpu.SemaphoreType.DMA((2, DEPTH)),
        ],
        input_output_aliases=aliases,
        compiler_params=pltpu.CompilerParams(vmem_limit_bytes=60 * 2**20),
        cost_estimate=pl.CostEstimate(flops=2 * batch * dim * cols, bytes_accessed=76 * 2**20, transcendentals=0),
        name=f"attn{layer}",
    )(*args)


CW = 512
HALF = 128


def mlp_kernel(layer, att_ref, x_ref, norm_ref, wo_hbm, wg_hbm, wu_hbm, wd_hbm, out_ref,
               wo, wg, wu, wd, att, h, act, own, sd, sx, sg, rd, rx, ra,
               wsem, sd_sem, sx_sem, sg_sem, rd_sem, rx_sem, ra_sem):
    dim = x_ref.shape[1]
    nch = dim // 2 // CW
    tp = lax.axis_index("tp")
    core = lax.rem(tp, 2)
    sib = tp + 1 - 2 * core
    peer = lax.rem(tp + 2, 4)
    mine = pl.multiple_of(core * (dim // 2), CW)
    theirs = pl.multiple_of((1 - core) * (dim // 2), CW)

    loads = []
    for idx, (src, dst) in enumerate(((wo_hbm, wo), (wg_hbm, wg), (wu_hbm, wu), (wd_hbm, wd))):
        loads.append(pltpu.make_async_copy(src.at[layer], dst, wsem.at[idx]))
    for c in loads:
        c.start()

    barrier = pltpu.get_barrier_semaphore()
    for other in (sib, peer):
        pl.semaphore_signal(barrier, inc=1, device_id={"tp": other}, device_id_type=MESH)
    pl.semaphore_wait(barrier, 2)

    out_ref[...] = x_ref[...]

    def to_sib(ph, k):
        return pltpu.make_async_remote_copy(sd.at[ph % 2, k], rd.at[ph, k], sd_sem.at[ph, k], rd_sem.at[ph, k],
                                            device_id={"tp": sib}, device_id_type=MESH)

    def to_peer(ph, k):
        return pltpu.make_async_remote_copy(sx.at[ph % 2, k], rx.at[ph, k], sx_sem.at[ph, k], rx_sem.at[ph, k],
                                            device_id={"tp": peer}, device_id_type=MESH)

    def share(ph, k):
        return pltpu.make_async_remote_copy(sg.at[ph % 2, k], ra.at[ph, k], sg_sem.at[ph, k], ra_sem.at[ph, k],
                                            device_id={"tp": sib}, device_id_type=MESH)

    def reduce_start(ph, lhs_ref, w_ref):
        for k in range(nch):
            sd[ph % 2, k] = jnp.dot(lhs_ref[...], w_ref[:, pl.ds(theirs + k * CW, CW)], preferred_element_type=F32).astype(BF)
            to_sib(ph, k).start()
        for k in range(nch):
            own[k] = jnp.dot(lhs_ref[...], w_ref[:, pl.ds(mine + k * CW, CW)], preferred_element_type=F32)
            to_sib(ph, k).wait_recv()
            sx[ph % 2, k] = (own[k] + rd[ph, k].astype(F32)).astype(BF)
            to_peer(ph, k).start()
        for k in range(nch):
            to_sib(ph, k).wait_send()

    def reduce_end(ph):
        rows = pl.ds((ph % 2) * HALF, HALF)
        for k in range(nch):
            to_peer(ph, k).wait()
            total = (sx[ph % 2, k].astype(F32) + rx[ph, k].astype(F32)).astype(BF)
            sg[ph % 2, k] = total
            share(ph, k).start()
            cols = pl.ds(mine + k * CW, CW)
            out_ref[rows, cols] = (out_ref[rows, cols].astype(F32) + total.astype(F32)).astype(BF)
        for k in range(nch):
            share(ph, k).wait()
            cols = pl.ds(theirs + k * CW, CW)
            out_ref[rows, cols] = (out_ref[rows, cols].astype(F32) + ra[ph, k].astype(F32)).astype(BF)

    def mlp(half):
        rows = pl.ds(half * HALF, HALF)
        h[...] = normed(out_ref[rows, :].astype(F32), norm_ref[layer:layer + 1, :].astype(F32))

        @pl.loop(0, act.shape[1] // 256)
        def _(n):
            cols = pl.ds(pl.multiple_of(n * 256, 256), 256)
            g = jnp.dot(h[...], wg[:, cols], preferred_element_type=F32).astype(BF).astype(F32)
            u = jnp.dot(h[...], wu[:, cols], preferred_element_type=F32).astype(BF).astype(F32)
            act[:, cols] = (g * jax.nn.sigmoid(g) * u).astype(BF)

    loads[0].wait()
    for half in range(2):
        for j in range(att.shape[1] // 128):
            att[:, j * 128:(j + 1) * 128] = att_ref[pl.ds(half * HALF * 8 + j, HALF, stride=8), :].astype(BF)
        reduce_start(half, att, wo)
    for half in range(2):
        reduce_end(half)
        if half == 0:
            loads[1].wait()
            loads[2].wait()
        mlp(half)
        if half == 0:
            loads[3].wait()
        reduce_start(2 + half, act, wd)
    for half in range(2):
        reduce_end(2 + half)


def mlp_block(layer, att, hidden, norm, wo, wg, wu, wd):
    batch, dim = hidden.shape
    nch = dim // 2 // CW
    anyspec = pl.BlockSpec(memory_space=pl.ANY)
    vmem = pl.BlockSpec(memory_space=pltpu.VMEM)
    msg = lambda n: pltpu.VMEM((n, nch, HALF, CW), BF)
    sems = pltpu.SemaphoreType.DMA((4, nch))
    return pl.pallas_call(
        functools.partial(mlp_kernel, layer),
        out_shape=jax.ShapeDtypeStruct((batch, dim), BF),
        in_specs=[vmem, vmem, vmem] + [anyspec] * 4,
        out_specs=vmem,
        scratch_shapes=[
            pltpu.VMEM(wo.shape[1:], BF), pltpu.VMEM(wg.shape[1:], BF), pltpu.VMEM(wu.shape[1:], BF), pltpu.VMEM(wd.shape[1:], BF),
            pltpu.VMEM((HALF, wo.shape[1]), BF), pltpu.VMEM((HALF, dim), BF), pltpu.VMEM((HALF, wd.shape[1]), BF),
            pltpu.VMEM((nch, HALF, CW), F32),
            msg(2), msg(2), msg(2), msg(4), msg(4), msg(4),
            pltpu.SemaphoreType.DMA((4,)), sems, sems, sems, sems, sems, sems,
        ],
        compiler_params=pltpu.CompilerParams(collective_id=layer, has_side_effects=True, vmem_limit_bytes=62 * 2**20),
        name=f"mlp{layer}",
    )(att, hidden, norm, wo, wg, wu, wd)


def solution(mesh):
    row_spec = P('dp', None)
    pos_spec = P('dp')
    cache_spec = P(None, 'dp', None, 'tp', None)
    norm_spec = P(None, None)
    col_spec = P(None, None, 'tp')
    split_rows = P(None, 'tp', None)

    def local_step(hidden, positions, k_cache, v_cache, attn_norm, w_query, w_key, w_value, w_out, mlp_norm, w_gate, w_up, w_down):
        cache_shape = k_cache.shape
        flat = (cache_shape[0], cache_shape[1], cache_shape[2] * cache_shape[3], cache_shape[4])
        k_flat, v_flat = k_cache.reshape(flat), v_cache.reshape(flat)
        cos_f, sin_f = rope_full(positions, cache_shape[4])
        caches = None
        for layer in range(cache_shape[0]):
            att, *caches = attention(layer, positions, hidden, attn_norm, cos_f, sin_f, w_query, w_key, w_value, k_flat, v_flat, caches)
            hidden = mlp_block(layer, att, hidden, mlp_norm, w_out, w_gate, w_up, w_down)
        return hidden, caches[0].reshape(cache_shape), caches[1].reshape(cache_shape)

    return jax.shard_map(local_step, mesh=mesh, in_specs=(row_spec, pos_spec, cache_spec, cache_spec, norm_spec, col_spec, col_spec, col_spec, split_rows, norm_spec, col_spec, col_spec, split_rows), out_specs=(row_spec, cache_spec, cache_spec), check_vma=False)
```

time: 423 us -> 226 us (0.53); the launches traced: 417 us -> 225 us
  Pallas kernels: 0 us -> 220 us
  matrix products: 118 us -> 0 us
  waiting for transfers between devices: 113 us -> 0 us
  other arithmetic: 104 us -> 2.09 us
  local copies, waits for them, and re-layouts: 67.1 us -> 2.65 us
  between operations: 14.8 us -> 0.67 us
    pallas_call x0 -> x4, Pallas kernels: none -> 220 us  [the longest x2 122 us: attention(): pl.pallas_call(functools.partial(attn_kernel, layer, prev is not None), o...]
    dot_general x16 -> x0, matrix products: 118 us -> none  [the longest x2 32.4 us: mlp_block(): jnp.dot(activated, wd_layer, preferred_element_type=jnp.float32)]
    psum x4 -> x0, waiting for transfers between devices: 113 us -> none  [local_step(): hidden = hidden + lax.psum(part_out, 'tp')]
    select_n x2 -> x1, other arithmetic: 79.6 us -> 0.02 us  [rope_full(): jnp.where(wavelen < 2048.0, inv_freq, jnp.where(wavelen > 8192.0, inv_fre...]
    slice x2 -> x0, local copies, waits for them, and re-layouts: 54 us -> none  [the longest x1 28 us: local_step(): k_cache[layer]]
    reduce_sum x6 -> x0, other arithmetic: 13.5 us -> none  [the longest x4 8.52 us: rms_norm(): mean_sq = jnp.mean(hidden_f32 * hidden_f32, axis=-1, keepdims=True)]
    convert_element_type x8 -> x0, local copies, waits for them, and re-layouts: 6.34 us -> none  [the longest x2 2.79 us: apply_rope(): vec_f32 = vectors.astype(jnp.float32)]
  transfers between devices with their start and end apart: 4 -> 0, of which waited for: 3 -> 0; matrix products, arithmetic and copies ran while one was open for 19% -> 0% of each run, Pallas kernels for 0% -> 0%
where the time goes in v1:
time: 226 us; the launch traced here: 225 us
  Pallas kernels  220 us (97%)
  local copies, waits for them, and re-layouts  2.65 us (1%)
    pallas_call x2, Pallas kernels, attention(): pl.pallas_call(functools.partial(attn_kernel, layer, prev is not None), o...  122 us
    pallas_call x2, Pallas kernels, mlp_block(): pl.pallas_call(functools.partial(mlp_kernel, layer), out_shape=jax.ShapeD...  98.2 us

profile of v1, /device:TPU:0, one launch (start us, length us, event | category | flops | bytes accessed | tf_op | source)
XLA Modules:
  0.0 225.4 jit_solution(10053717157122373227)
XLA Ops:
  0.7 0.7 convert_element_type.3
  1.3 0.5 fusion
  1.9 0.8 pad_maximum_fusion
  2.7 60.9 %attn0.1 = (f32[2048,128]{1,0:T(8,128)}, bf16[2,256,256,128]{3,2,1,0:T(8,128)(2,1)}, bf16[2,256,256,128]{3,2,1,0:T(8,128)(2,1)}) custom-call(s32[256]{0:T(256)} %pos_ref.3, bf16[256,3072]{1,0:T(8,128)(2,1)} %x_ref.3, bf16[2,3072]{1,0:T(2,128)(2,1)} %norm_ref.6, f32[256,128]{1,0:T(8,128)} %get-tuple-element.18.cos_ref, f32[256,128]{1,0:T(8,128)} %get-tuple-element.19.sin_ref, ...), custom_call_target="tpu_custom_call" | custom-call | flops 2013265920 | bytes 79691776 | tf_op jit(solution)/shard_map/attn0/pallas_call | solution.py:168
  63.6 49.5 %mlp0.1.x_ref = bf16[256,3072]{1,0:T(8,128)(2,1)} custom-call(f32[2048,128]{1,0:T(8,128)} %get-tuple-element.9.att_ref, bf16[256,3072]{1,0:T(8,128)(2,1)} %x_ref.3, bf16[2,3072]{1,0:T(2,128)(2,1)} %norm_ref.7, bf16[2,768,3072]{2,1,0:T(8,128)(2,1)} %wo_hbm.3, bf16[2,3072,2048]{2,1,0:T(8,128)(2,1)} %wg_hbm.3, bf16[2,3072,2048]{2,1,0:T(8,128)(2,1)} %wu_hbm.3, ...), custom_call_target="tpu_custom_call" | custom-call | tf_op jit(solution)/shard_map/mlp0/pallas_call | solution.py:297
  113.1 60.9 %attn1.1 = (f32[2048,128]{1,0:T(8,128)}, bf16[2,256,256,128]{3,2,1,0:T(8,128)(2,1)}, bf16[2,256,256,128]{3,2,1,0:T(8,128)(2,1)}) custom-call(s32[256]{0:T(256)} %pos_ref.3, bf16[256,3072]{1,0:T(8,128)(2,1)} %mlp0.1.x_ref, bf16[2,3072]{1,0:T(2,128)(2,1)} %norm_ref.6, ...), custom_call_target="tpu_custom_call", output_to_operand_aliasing={{1}: (10, {}), {2}: (11, {})} | custom-call | flops 2013265920 | bytes 79691776 | tf_op jit(solution)/shard_map/attn1/pallas_call | solution.py:168
  174.0 48.7 %mlp1.1 = bf16[256,3072]{1,0:T(8,128)(2,1)} custom-call(f32[2048,128]{1,0:T(8,128)} %get-tuple-element.12.att_ref, bf16[256,3072]{1,0:T(8,128)(2,1)} %mlp0.1.x_ref, bf16[2,3072]{1,0:T(2,128)(2,1)} %norm_ref.7, bf16[2,768,3072]{2,1,0:T(8,128)(2,1)} %wo_hbm.3, bf16[2,3072,2048]{2,1,0:T(8,128)(2,1)} %wg_hbm.3, bf16[2,3072,2048]{2,1,0:T(8,128)(2,1)} %wu_hbm.3, ...), custom_call_target="tpu_custom_call" | custom-call | tf_op jit(solution)/shard_map/mlp1/pallas_call | solution.py:297
  222.7 2.7 %copy.21 = bf16[256,3072]{1,0:T(8,128)(2,1)} copy(bf16[256,3072]{1,0:T(8,128)(2,1)} %mlp1.1) | data formatting | bytes 3145728
  (1 shorter events, 0.0 us)

commit v2 on v1

v2 whole, which is shorter than its diff:
```python
import functools
import math
import jax
import jax.numpy as jnp
import numpy as np
from jax import lax
from jax.experimental import pallas as pl
from jax.experimental.pallas import tpu as pltpu
from jax.sharding import PartitionSpec as P

BF = jnp.bfloat16
F32 = jnp.float32
MESH = pl.DeviceIdType.MESH
EPS = 1e-5
NEG = -1e30


def rope_table(rows, head_dim):
    half_dim = head_dim // 2
    inv_freq = np.power(np.float32(500000.0), -np.arange(half_dim, dtype=np.float32) * np.float32(2.0 / head_dim)).astype(np.float32)
    wavelen = (np.float32(2.0 * math.pi) / inv_freq).astype(np.float32)
    smooth = (np.float32(8192.0) / wavelen - np.float32(1.0)) / np.float32(3.0)
    blended = (np.float32(1.0) - smooth) * inv_freq / np.float32(8.0) + smooth * inv_freq
    scaled = np.where(wavelen < 2048.0, inv_freq, np.where(wavelen > 8192.0, inv_freq / np.float32(8.0), blended)).astype(np.float32)
    angles = np.arange(rows, dtype=np.float32)[:, None] * scaled[None, :]
    cos, sin = np.cos(angles.astype(np.float64)), np.sin(angles.astype(np.float64))
    return np.concatenate([cos, cos, -sin, sin], axis=-1).astype(np.float32)


def normed(x_f32, weight_f32):
    mean_sq = jnp.mean(x_f32 * x_f32, axis=-1, keepdims=True)
    return (x_f32 * lax.rsqrt(mean_sq + EPS) * weight_f32).astype(BF)


BLK = 16


def attn_kernel(layer, has_qkv, aliased, *refs):
    pos_hbm, table_hbm = refs[:2]
    if has_qkv:
        qkv_hbm, k_hbm, v_hbm = refs[2:5]
        refs = refs[5:]
    else:
        x_hbm, norm_hbm, wq_hbm, wk_hbm, wv_hbm, k_hbm, v_hbm = refs[2:9]
        refs = refs[9:]
    if aliased:
        refs = refs[2:]
    att_hbm, ko_hbm, vo_hbm, pos_ref, table, qkv, cs, q_rows, k_rows, v_rows, o_rows, att, kbuf, vbuf, sem, insem, outsem, *rest = refs
    nblk = kbuf.shape[0]
    batch = nblk * BLK
    heads = att.shape[1] // 128

    pos_copy = pltpu.make_async_copy(pos_hbm, pos_ref, sem.at[0])
    table_copy = pltpu.make_async_copy(table_hbm, table, sem.at[1])
    pos_copy.start()
    table_copy.start()
    if has_qkv:
        first = [pltpu.make_async_copy(qkv_hbm, qkv, sem.at[2])]
    else:
        x_buf, norm, w_buf, h_buf = rest
        qcols = wq_hbm.shape[2]
        kcols = wk_hbm.shape[2]
        x_copies = [pltpu.make_async_copy(x_hbm, x_buf, sem.at[3]), pltpu.make_async_copy(norm_hbm, norm, sem.at[4])]
        for c in x_copies:
            c.start()
        first = [
            pltpu.make_async_copy(wq_hbm.at[layer], w_buf.at[:, pl.ds(0, qcols)], sem.at[5]),
            pltpu.make_async_copy(wk_hbm.at[layer], w_buf.at[:, pl.ds(qcols, kcols)], sem.at[6]),
            pltpu.make_async_copy(wv_hbm.at[layer], w_buf.at[:, pl.ds(qcols + kcols, kcols)], sem.at[7]),
        ]
    for c in first:
        c.start()

    def in_copies(i):
        rows = pl.ds(i * BLK, BLK)
        return (pltpu.make_async_copy(k_hbm.at[layer, rows], kbuf.at[i], insem.at[0, i]),
                pltpu.make_async_copy(v_hbm.at[layer, rows], vbuf.at[i], insem.at[1, i]))

    def out_copies(i):
        rows = pl.ds(i * BLK, BLK)
        return (pltpu.make_async_copy(kbuf.at[i], ko_hbm.at[layer, rows], outsem.at[0, i]),
                pltpu.make_async_copy(vbuf.at[i], vo_hbm.at[layer, rows], outsem.at[1, i]))

    @pl.loop(0, nblk)
    def _(i):
        for c in in_copies(i):
            c.start()

    pos_copy.wait()
    table_copy.wait()

    @pl.loop(0, batch // 8)
    def _(i):
        for b in range(8):
            r = i * 8 + b
            cs[pl.ds(r, 1), :] = table[pl.ds(pos_ref[r], 1), :]

    if not has_qkv:
        for c in x_copies:
            c.wait()
        h_buf[...] = normed(x_buf[...].astype(F32), norm[layer:layer + 1, :].astype(F32))
    for c in first:
        c.wait()
    if not has_qkv:
        @pl.loop(0, (qcols + 2 * kcols) // 256)
        def _(n):
            cols = pl.ds(pl.multiple_of(n * 256, 256), 256)
            qkv[n] = jnp.dot(h_buf[...], w_buf[:, cols], preferred_element_type=F32).astype(BF)

    cos_b = cs[:, 0:128]
    sin_b = cs[:, 128:256]

    def piece(n, h):
        return qkv[n, :, h * 128:h * 128 + 128].astype(F32)

    def rope(vec):
        return (vec * cos_b + pltpu.roll(vec, 64, 1) * sin_b).astype(BF).astype(F32)

    zero = jnp.zeros((batch, 128), F32)
    for j in range(8):
        q_rows[pl.ds(j, batch, stride=8), :] = rope(piece(j // 2, j % 2)) if j < heads else zero
    for h in range(2):
        k_vec = rope(piece(heads // 2, h))
        v_vec = piece(heads // 2 + 1, h)
        for r in range(4):
            k_rows[pl.ds(2 * r + h, batch, stride=8), :] = k_vec
            v_rows[pl.ds(2 * r + h, batch, stride=8), :] = v_vec

    col = lax.broadcasted_iota(jnp.int32, (8, 256), 1)
    row = lax.broadcasted_iota(jnp.int32, (8, 256), 0)
    own = (col & 1) == jnp.where(row >= heads // 2, 1, 0)
    key_row = jnp.where(own, col >> 1, 4096)
    seq_in_group = lax.broadcasted_iota(jnp.int32, (16, 128), 0) >> 1
    scale = 128 ** -0.5

    @pl.loop(0, nblk)
    def _(i):
        for c in in_copies(i):
            c.wait()
        for b in range(BLK):
            pos = pos_ref[i * BLK + b]
            group = pl.ds(pl.multiple_of((pos >> 3) * 16, 16), 16)
            hit = seq_in_group == (pos & 7)
            rows = pl.ds(pl.multiple_of((i * BLK + b) * 8, 8), 8)
            for buf, new in ((kbuf, k_rows), (vbuf, v_rows)):
                new8 = new[rows, :]
                new16 = jnp.concatenate([new8, new8], axis=0)
                old16 = buf[i, b, group, :].astype(F32)
                buf[i, b, group, :] = jnp.where(hit, new16, old16).astype(BF)
        zero8 = jnp.zeros((8, 128), F32)
        pairs = range(BLK // 2)
        scores = []
        for p in pairs:
            first = i * BLK + 2 * p
            qa = q_rows[pl.ds(pl.multiple_of(first * 8, 8), 8), :]
            qb = q_rows[pl.ds(pl.multiple_of(first * 8 + 8, 8), 8), :]
            q2 = jnp.concatenate([jnp.concatenate([qa, zero8], axis=1), jnp.concatenate([zero8, qb], axis=1)], axis=0).astype(BF)
            k2 = jnp.concatenate([kbuf[i, 2 * p], kbuf[i, 2 * p + 1]], axis=1)
            scores.append(lax.dot_general(q2, k2, (((1,), (1,)), ((), ())), preferred_element_type=F32))
        weights = []
        for p in pairs:
            first = i * BLK + 2 * p
            keep = jnp.concatenate([key_row <= pos_ref[first], key_row <= pos_ref[first + 1]], axis=0)
            s = jnp.where(keep, scores[p] * scale, NEG)
            e = jnp.exp(s - jnp.max(s, axis=-1, keepdims=True))
            weights.append((e * (1.0 / jnp.sum(e, axis=-1, keepdims=True))).astype(BF))
        outs = []
        for p in pairs:
            v2 = jnp.concatenate([vbuf[i, 2 * p], vbuf[i, 2 * p + 1]], axis=1)
            outs.append(jnp.dot(weights[p], v2, preferred_element_type=F32))
        for c in out_copies(i):
            c.start()
        for p in pairs:
            o_rows[16 * p:16 * p + 8, :] = outs[p][0:8, 0:128]
            o_rows[16 * p + 8:16 * p + 16, :] = outs[p][8:16, 128:256]
        rows = pl.ds(pl.multiple_of(i * BLK, BLK), BLK)
        for j in range(heads):
            att[rows, j * 128:(j + 1) * 128] = o_rows[pl.ds(j, BLK, stride=8), :].astype(BF)

    att_copy = pltpu.make_async_copy(att, att_hbm, sem.at[8])
    att_copy.start()
    att_copy.wait()

    @pl.loop(0, nblk)
    def _(i):
        for c in out_copies(i):
            c.wait()


def attention(layer, positions, table, source, k_cache, v_cache, prev, qcols, kcols):
    batch = positions.shape[0]
    has_qkv = len(source) == 1
    anyspec = pl.BlockSpec(memory_space=pl.ANY)
    args = [positions, table, *source, k_cache, v_cache]
    aliases = {}
    if prev is not None:
        aliases = {len(args): 1, len(args) + 1: 2}
        args += list(prev)
    cols = qcols + 2 * kcols
    nblk = batch // BLK
    scratch = [
        pltpu.SMEM((batch,), jnp.int32),
        pltpu.VMEM(table.shape, F32),
        pltpu.VMEM((cols // 256, batch, 256), BF),
        pltpu.VMEM((batch, table.shape[1]), F32),
        pltpu.VMEM((batch * 8, 128), F32),
        pltpu.VMEM((batch * 8, 128), F32),
        pltpu.VMEM((batch * 8, 128), F32),
        pltpu.VMEM((BLK * 8, 128), F32),
        pltpu.VMEM((batch, qcols), BF),
        pltpu.VMEM((nblk, BLK) + k_cache.shape[2:], BF),
        pltpu.VMEM((nblk, BLK) + v_cache.shape[2:], BF),
        pltpu.SemaphoreType.DMA((9,)),
        pltpu.SemaphoreType.DMA((2, nblk)),
        pltpu.SemaphoreType.DMA((2, nblk)),
    ]
    if not has_qkv:
        hidden, norm = source[:2]
        dim = hidden.shape[1]
        scratch += [pltpu.VMEM(hidden.shape, BF), pltpu.VMEM(norm.shape, BF), pltpu.VMEM((dim, cols), BF), pltpu.VMEM(hidden.shape, BF)]
    return pl.pallas_call(
        functools.partial(attn_kernel, layer, has_qkv, prev is not None),
        out_shape=(jax.ShapeDtypeStruct((batch, qcols), BF),
                   jax.ShapeDtypeStruct(k_cache.shape, BF), jax.ShapeDtypeStruct(v_cache.shape, BF)),
        in_specs=[anyspec] * len(args),
        out_specs=(anyspec, anyspec, anyspec),
        scratch_shapes=scratch,
        input_output_aliases=aliases,
        compiler_params=pltpu.CompilerParams(vmem_limit_bytes=62 * 2**20),
        cost_estimate=pl.CostEstimate(flops=2 * batch * 3072 * cols, bytes_accessed=76 * 2**20, transcendentals=0),
        name=f"attn{layer}",
    )(*args)


CW = 512
HALF = 128
GW = 512


def mlp_kernel(layer, next_qkv, att_hbm, x_hbm, norm_hbm, wo_hbm, wg_hbm, wu_hbm, wd_hbm, *refs):
    if next_qkv:
        norm2_hbm, wq_hbm, wk_hbm, wv_hbm, out_hbm, qkv_hbm = refs[:6]
        refs = refs[6:]
    else:
        out_hbm = refs[0]
        refs = refs[1:]
    (wo, wg, wu, wd, att, x, norm, h, act, sd, sx, sg, rd, rx, ra,
     wsem, isem, sd_sem, sx_sem, sg_sem, rd_sem, rx_sem, ra_sem, *refs) = refs
    dim = x.shape[1]
    nch = dim // 2 // CW
    tp = lax.axis_index("tp")
    core = lax.rem(tp, 2)
    sib = tp + 1 - 2 * core
    peer = lax.rem(tp + 2, 4)
    mine = pl.multiple_of(core * (dim // 2), CW)
    theirs = pl.multiple_of((1 - core) * (dim // 2), CW)

    half_rows = wo.shape[0] // 2
    att_copy = pltpu.make_async_copy(att_hbm, att, isem.at[0])
    wo_copies = [pltpu.make_async_copy(wo_hbm.at[layer, pl.ds(r * half_rows, half_rows)], wo.at[pl.ds(r * half_rows, half_rows)], wsem.at[r]) for r in range(2)]
    x_copy = pltpu.make_async_copy(x_hbm, x, isem.at[1])
    norm_copy = pltpu.make_async_copy(norm_hbm, norm, isem.at[2])
    wg_copy = pltpu.make_async_copy(wg_hbm.at[layer], wg, wsem.at[2])
    wu_copy = pltpu.make_async_copy(wu_hbm.at[layer], wu, wsem.at[3])
    wd_copy = pltpu.make_async_copy(wd_hbm.at[layer], wd, wsem.at[4])
    for c in [att_copy, *wo_copies]:
        c.start()
    if next_qkv:
        norm2, wqkv, qkv = refs
        qcols = wq_hbm.shape[2]
        kcols = wk_hbm.shape[2]
        qkv_loads = [
            pltpu.make_async_copy(norm2_hbm, norm2, isem.at[3]),
            pltpu.make_async_copy(wq_hbm.at[layer + 1], wqkv.at[:, pl.ds(0, qcols)], wsem.at[5]),
            pltpu.make_async_copy(wk_hbm.at[layer + 1], wqkv.at[:, pl.ds(qcols, kcols)], wsem.at[6]),
            pltpu.make_async_copy(wv_hbm.at[layer + 1], wqkv.at[:, pl.ds(qcols + kcols, kcols)], wsem.at[7]),
        ]

    barrier = pltpu.get_barrier_semaphore()
    for other in (sib, peer):
        pl.semaphore_signal(barrier, inc=1, device_id={"tp": other}, device_id_type=MESH)
    pl.semaphore_wait(barrier, 2)

    def to_sib(ph, k):
        return pltpu.make_async_remote_copy(sd.at[ph % 2, k], rd.at[ph, k], sd_sem.at[ph, k], rd_sem.at[ph, k],
                                            device_id={"tp": sib}, device_id_type=MESH)

    def to_peer(ph, k):
        return pltpu.make_async_remote_copy(sx.at[ph % 2, k], rx.at[ph, k], sx_sem.at[ph, k], rx_sem.at[ph, k],
                                            device_id={"tp": peer}, device_id_type=MESH)

    def share(ph, k):
        return pltpu.make_async_remote_copy(sg.at[ph % 2, k], ra.at[ph, k], sg_sem.at[ph, k], ra_sem.at[ph, k],
                                            device_id={"tp": sib}, device_id_type=MESH)

    def reduce_start(ph, lhs, w_ref):
        for k in range(nch):
            sd[ph % 2, k] = jnp.dot(lhs, w_ref[:, pl.ds(theirs + k * CW, CW)], preferred_element_type=F32).astype(BF)
            to_sib(ph, k).start()
        for k in range(nch):
            part = jnp.dot(lhs, w_ref[:, pl.ds(mine + k * CW, CW)], preferred_element_type=F32)
            to_sib(ph, k).wait_recv()
            sx[ph % 2, k] = (part + rd[ph, k].astype(F32)).astype(BF)
            to_peer(ph, k).start()
        for k in range(nch):
            to_sib(ph, k).wait_send()

    def reduce_end(ph):
        rows = pl.ds((ph % 2) * HALF, HALF)
        for k in range(nch):
            to_peer(ph, k).wait()
            total = (sx[ph % 2, k].astype(F32) + rx[ph, k].astype(F32)).astype(BF)
            sg[ph % 2, k] = total
            share(ph, k).start()
            cols = pl.ds(mine + k * CW, CW)
            x[rows, cols] = (x[rows, cols].astype(F32) + total.astype(F32)).astype(BF)
        for k in range(nch):
            share(ph, k).wait()
            cols = pl.ds(theirs + k * CW, CW)
            x[rows, cols] = (x[rows, cols].astype(F32) + ra[ph, k].astype(F32)).astype(BF)

    def mlp(half):
        rows = pl.ds(half * HALF, HALF)
        h[...] = normed(x[rows, :].astype(F32), norm[layer:layer + 1, :].astype(F32))

        @pl.loop(0, act.shape[1] // GW)
        def _(n):
            cols = pl.ds(pl.multiple_of(n * GW, GW), GW)
            g = jnp.dot(h[...], wg[:, cols], preferred_element_type=F32).astype(BF).astype(F32)
            u = jnp.dot(h[...], wu[:, cols], preferred_element_type=F32).astype(BF).astype(F32)
            act[:, cols] = (g * jax.nn.sigmoid(g) * u).astype(BF)

    def out_copy(half):
        rows = pl.ds(half * HALF, HALF)
        return pltpu.make_async_copy(x.at[rows], out_hbm.at[rows], isem.at[4 + half])

    def qkv_copy(half):
        rows = pl.ds(half * HALF, HALF)
        return pltpu.make_async_copy(qkv.at[:, rows], qkv_hbm.at[:, rows], isem.at[6 + half])

    att_copy.wait()
    for c in wo_copies:
        c.wait()
    for c in (x_copy, norm_copy, wg_copy, wu_copy):
        c.start()
    for half in range(2):
        reduce_start(half, att[half * HALF:(half + 1) * HALF, :], wo)
    wd_copy.start()
    if next_qkv:
        for c in qkv_loads:
            c.start()
    x_copy.wait()
    norm_copy.wait()
    for half in range(2):
        reduce_end(half)
        if half == 0:
            wg_copy.wait()
            wu_copy.wait()
        mlp(half)
        if half == 0:
            wd_copy.wait()
        reduce_start(2 + half, act[...], wd)
    if next_qkv:
        for c in qkv_loads:
            c.wait()
    for half in range(2):
        rows = pl.ds(half * HALF, HALF)
        reduce_end(2 + half)
        out_copy(half).start()
        if next_qkv:
            h[...] = normed(x[rows, :].astype(F32), norm2[layer + 1:layer + 2, :].astype(F32))

            @pl.loop(0, qkv.shape[0])
            def _(n):
                cols = pl.ds(pl.multiple_of(n * 256, 256), 256)
                qkv[n, rows, :] = jnp.dot(h[...], wqkv[:, cols], preferred_element_type=F32).astype(BF)

            qkv_copy(half).start()
    for half in range(2):
        out_copy(half).wait()
        if next_qkv:
            qkv_copy(half).wait()


def mlp_block(layer, att, hidden, norm, wo, wg, wu, wd, following):
    batch, dim = hidden.shape
    nch = dim // 2 // CW
    anyspec = pl.BlockSpec(memory_space=pl.ANY)
    msg = lambda n: pltpu.VMEM((n, nch, HALF, CW), BF)
    sems = pltpu.SemaphoreType.DMA((4, nch))
    args = [att, hidden, norm, wo, wg, wu, wd]
    scratch = [
        pltpu.VMEM(wo.shape[1:], BF), pltpu.VMEM(wg.shape[1:], BF), pltpu.VMEM(wu.shape[1:], BF), pltpu.VMEM(wd.shape[1:], BF),
        pltpu.VMEM(att.shape, BF), pltpu.VMEM(hidden.shape, BF), pltpu.VMEM(norm.shape, BF),
        pltpu.VMEM((HALF, dim), BF), pltpu.VMEM((HALF, wd.shape[1]), BF),
        msg(2), msg(2), msg(2), msg(4), msg(4), msg(4),
        pltpu.SemaphoreType.DMA((8,)), pltpu.SemaphoreType.DMA((8,)), sems, sems, sems, sems, sems, sems,
    ]
    out_shape = [jax.ShapeDtypeStruct((batch, dim), BF)]
    if following is not None:
        norm2, wq, wk, wv = following
        args += list(following)
        cols = wq.shape[2] + 2 * wk.shape[2]
        out_shape.append(jax.ShapeDtypeStruct((cols // 256, batch, 256), BF))
        scratch += [pltpu.VMEM(norm2.shape, BF), pltpu.VMEM((dim, cols), BF), pltpu.VMEM((cols // 256, batch, 256), BF)]
    return pl.pallas_call(
        functools.partial(mlp_kernel, layer, following is not None),
        out_shape=out_shape,
        in_specs=[anyspec] * len(args),
        out_specs=[anyspec] * len(out_shape),
        scratch_shapes=scratch,
        compiler_params=pltpu.CompilerParams(collective_id=layer, has_side_effects=True, vmem_limit_bytes=67043328),
        name=f"mlp{layer}",
    )(*args)


def solution(mesh):
    row_spec = P('dp', None)
    pos_spec = P('dp')
    cache_spec = P(None, 'dp', None, 'tp', None)
    norm_spec = P(None, None)
    col_spec = P(None, None, 'tp')
    split_rows = P(None, 'tp', None)

    def local_step(hidden, positions, k_cache, v_cache, attn_norm, w_query, w_key, w_value, w_out, mlp_norm, w_gate, w_up, w_down):
        cache_shape = k_cache.shape
        flat = (cache_shape[0], cache_shape[1], cache_shape[2] * cache_shape[3], cache_shape[4])
        k_flat, v_flat = k_cache.reshape(flat), v_cache.reshape(flat)
        table = jnp.asarray(rope_table(cache_shape[2], cache_shape[4]))
        layers = cache_shape[0]
        caches = None
        source = (hidden, attn_norm, w_query, w_key, w_value)
        for layer in range(layers):
            att, *caches = attention(layer, positions, table, source, k_flat, v_flat, caches, w_query.shape[2], w_key.shape[2])
            following = (attn_norm, w_query, w_key, w_value) if layer + 1 < layers else None
            hidden, *source = mlp_block(layer, att, hidden, mlp_norm, w_out, w_gate, w_up, w_down, following)
        return hidden, caches[0].reshape(cache_shape), caches[1].reshape(cache_shape)

    return jax.shard_map(local_step, mesh=mesh, in_specs=(row_spec, pos_spec, cache_spec, cache_spec, norm_spec, col_spec, col_spec, col_spec, split_rows, norm_spec, col_spec, col_spec, split_rows), out_specs=(row_spec, cache_spec, cache_spec), check_vma=False)
```

time: 226 us -> 147 us (0.65)
  Pallas kernels: 220 us -> 143 us
    pallas_call x4, Pallas kernels: 220 us -> 143 us  [the longest x2 93.9 us: mlp_block(): pl.pallas_call(functools.partial(mlp_kernel, layer, following is not None...]
where the time goes in v2:
time: 147 us; the launch traced here: 146 us
  Pallas kernels  143 us (97%)
  local copies, waits for them, and re-layouts  2.65 us (2%)
    pallas_call x2, Pallas kernels, mlp_block(): pl.pallas_call(functools.partial(mlp_kernel, layer, following is not None...  93.9 us
    pallas_call x2, Pallas kernels, attention(): pl.pallas_call(functools.partial(attn_kernel, layer, has_qkv, prev is not...  49.2 us

profile of v2, /device:TPU:0, one launch (start us, length us, event | category | flops | bytes accessed | tf_op | source)
XLA Modules:
  0.0 146.4 jit_solution(4097090694635354162)
XLA Ops:
  0.6 25.7 %attn0.1 = (bf16[256,768]{1,0:T(8,128)(2,1)}, bf16[2,256,256,128]{3,2,1,0:T(8,128)(2,1)}, bf16[2,256,256,128]{3,2,1,0:T(8,128)(2,1)}) custom-call(s32[256]{0:T(256)} %refs_0_.5, f32[128,256]{1,0:T(8,128)} %constant.2.clone.refs_1_, bf16[256,3072]{1,0:T(8,128)(2,1)} %x_hbm.1, bf16[2,3072]{1,0:T(2,128)(2,1)} %refs_0_.4, bf16[2,3072,768]{2,1,0:T(8,128)(2,1)} %refs_1_.3, ...), custom_call_target="tpu_custom_call" | custom-call | flops 2013265920 | bytes 79691776 | tf_op jit(solution)/shard_map/attn0/pallas_call | solution.py:221
  26.3 48.3 %mlp0.1 = (bf16[256,3072]{1,0:T(8,128)(2,1)}, bf16[5,256,256]{2,1,0:T(8,128)(2,1)}) custom-call(bf16[256,768]{1,0:T(8,128)(2,1)} %get-tuple-element.11.att_hbm, bf16[256,3072]{1,0:T(8,128)(2,1)} %x_hbm.1, bf16[2,3072]{1,0:T(2,128)(2,1)} %norm_hbm.3, bf16[2,768,3072]{2,1,0:T(8,128)(2,1)} %wo_hbm.3, bf16[2,3072,2048]{2,1,0:T(8,128)(2,1)} %wg_hbm.3, ...), custom_call_target="tpu_custom_call" | custom-call | tf_op jit(solution)/shard_map/mlp0/pallas_call | solution.py:406
  74.6 23.6 %attn1.1 = (bf16[256,768]{1,0:T(8,128)(2,1)}, bf16[2,256,256,128]{3,2,1,0:T(8,128)(2,1)}, bf16[2,256,256,128]{3,2,1,0:T(8,128)(2,1)}) custom-call(s32[256]{0:T(256)} %refs_0_.5, f32[128,256]{1,0:T(8,128)} %constant.2.clone.refs_1_, bf16[5,256,256]{2,1,0:T(8,128)(2,1)} %get-tuple-element.12.refs_2_, ...), custom_call_target="tpu_custom_call", output_to_operand_aliasing={{1}: (5, {}), {2}: (6, {})} | custom-call | flops 2013265920 | bytes 79691776 | tf_op jit(solution)/shard_map/attn1/pallas_call | solution.py:221
  98.2 45.5 %mlp1.1 = bf16[256,3072]{1,0:T(8,128)(2,1)} custom-call(bf16[256,768]{1,0:T(8,128)(2,1)} %get-tuple-element.15.att_hbm, bf16[256,3072]{1,0:T(8,128)(2,1)} %get-tuple-element.16.x_hbm, bf16[2,3072]{1,0:T(2,128)(2,1)} %norm_hbm.3, bf16[2,768,3072]{2,1,0:T(8,128)(2,1)} %wo_hbm.3, bf16[2,3072,2048]{2,1,0:T(8,128)(2,1)} %wg_hbm.3, bf16[2,3072,2048]{2,1,0:T(8,128)(2,1)} %wu_hbm.3, ...), custom_call_target="tpu_custom_call" | custom-call | tf_op jit(solution)/shard_map/mlp1/pallas_call | solution.py:406
  143.8 2.7 %copy.22 = bf16[256,3072]{1,0:T(8,128)(2,1)} copy(bf16[256,3072]{1,0:T(8,128)(2,1)} %mlp1.1) | data formatting | bytes 3145728

commit v3 on v2

--- a/solution.py
+++ b/solution.py
@@ -33,6 +33,7 @@
 
 
 BLK = 16
+HOLD = 4
 
 
 def attn_kernel(layer, has_qkv, aliased, *refs):
@@ -168,8 +169,19 @@
         for p in pairs:
             v2 = jnp.concatenate([vbuf[i, 2 * p], vbuf[i, 2 * p + 1]], axis=1)
             outs.append(jnp.dot(weights[p], v2, preferred_element_type=F32))
-        for c in out_copies(i):
-            c.start()
+
+        @pl.when(i == HOLD)
+        def _():
+            @pl.loop(0, HOLD)
+            def _(j):
+                for c in out_copies(j):
+                    c.start()
+
+        @pl.when(i >= HOLD)
+        def _():
+            for c in out_copies(i):
+                c.start()
+
         for p in pairs:
             o_rows[16 * p:16 * p + 8, :] = outs[p][0:8, 0:128]
             o_rows[16 * p + 8:16 * p + 16, :] = outs[p][8:16, 128:256]
@@ -232,22 +244,118 @@
     )(*args)
 
 
+COPY_HOLD = 9
+
+
+def write_kernel(layer, pos_hbm, new_hbm, k_hbm, v_hbm, k_prev, v_prev, ko_hbm, vo_hbm, pos_ref, new, k_rows, v_rows, kbuf, vbuf, sem, insem, outsem):
+    nblk = kbuf.shape[0]
+    batch = nblk * BLK
+    first = [pltpu.make_async_copy(pos_hbm, pos_ref, sem.at[0]), pltpu.make_async_copy(new_hbm, new, sem.at[1])]
+    for c in first:
+        c.start()
+
+    def in_copies(i):
+        rows = pl.ds(i * BLK, BLK)
+        return (pltpu.make_async_copy(k_hbm.at[layer, rows], kbuf.at[i], insem.at[0, i]),
+                pltpu.make_async_copy(v_hbm.at[layer, rows], vbuf.at[i], insem.at[1, i]))
+
+    def out_copies(i):
+        rows = pl.ds(i * BLK, BLK)
+        return (pltpu.make_async_copy(kbuf.at[i], ko_hbm.at[layer, rows], outsem.at[0, i]),
+                pltpu.make_async_copy(vbuf.at[i], vo_hbm.at[layer, rows], outsem.at[1, i]))
+
+    @pl.loop(0, nblk)
+    def _(i):
+        for c in in_copies(i):
+            c.start()
+
+    for c in first:
+        c.wait()
+    for h in range(2):
+        k_vec = new[h].astype(F32)
+        v_vec = new[2 + h].astype(F32)
+        for r in range(4):
+            k_rows[pl.ds(2 * r + h, batch, stride=8), :] = k_vec
+            v_rows[pl.ds(2 * r + h, batch, stride=8), :] = v_vec
+    seq_in_group = lax.broadcasted_iota(jnp.int32, (16, 128), 0) >> 1
+
+    @pl.loop(0, nblk)
+    def _(i):
+        for c in in_copies(i):
+            c.wait()
+        for b in range(BLK):
+            pos = pos_ref[i * BLK + b]
+            group = pl.ds(pl.multiple_of((pos >> 3) * 16, 16), 16)
+            hit = seq_in_group == (pos & 7)
+            rows = pl.ds(pl.multiple_of((i * BLK + b) * 8, 8), 8)
+            for buf, rows_ref in ((kbuf, k_rows), (vbuf, v_rows)):
+                new8 = rows_ref[rows, :]
+                new16 = jnp.concatenate([new8, new8], axis=0)
+                old16 = buf[i, b, group, :].astype(F32)
+                buf[i, b, group, :] = jnp.where(hit, new16, old16).astype(BF)
+
+        @pl.when(i == COPY_HOLD)
+        def _():
+            @pl.loop(0, COPY_HOLD)
+            def _(j):
+                for c in out_copies(j):
+                    c.start()
+
+        @pl.when(i >= COPY_HOLD)
+        def _():
+            for c in out_copies(i):
+                c.start()
+
+    @pl.loop(0, nblk)
+    def _(i):
+        for c in out_copies(i):
+            c.wait()
+
+
+def write_rows(layer, positions, new, k_cache, v_cache, prev):
+    batch = positions.shape[0]
+    nblk = batch // BLK
+    anyspec = pl.BlockSpec(memory_space=pl.ANY)
+    return pl.pallas_call(
+        functools.partial(write_kernel, layer),
+        out_shape=(jax.ShapeDtypeStruct(k_cache.shape, BF), jax.ShapeDtypeStruct(v_cache.shape, BF)),
+        in_specs=[anyspec] * 6,
+        out_specs=(anyspec, anyspec),
+        scratch_shapes=[
+            pltpu.SMEM((batch,), jnp.int32),
+            pltpu.VMEM(new.shape, BF),
+            pltpu.VMEM((batch * 8, 128), F32),
+            pltpu.VMEM((batch * 8, 128), F32),
+            pltpu.VMEM((nblk, BLK) + k_cache.shape[2:], BF),
+            pltpu.VMEM((nblk, BLK) + v_cache.shape[2:], BF),
+            pltpu.SemaphoreType.DMA((2,)),
+            pltpu.SemaphoreType.DMA((2, nblk)),
+            pltpu.SemaphoreType.DMA((2, nblk)),
+        ],
+        input_output_aliases={4: 0, 5: 1},
+        compiler_params=pltpu.CompilerParams(vmem_limit_bytes=67043328),
+        cost_estimate=pl.CostEstimate(flops=0, bytes_accessed=67 * 2**20, transcendentals=0),
+        name="write_rows",
+    )(positions, new, k_cache, v_cache, *prev)
+
+
 CW = 512
 HALF = 128
-GW = 512
-
-
-def mlp_kernel(layer, next_qkv, att_hbm, x_hbm, norm_hbm, wo_hbm, wg_hbm, wu_hbm, wd_hbm, *refs):
-    if next_qkv:
-        norm2_hbm, wq_hbm, wk_hbm, wv_hbm, out_hbm, qkv_hbm = refs[:6]
-        refs = refs[6:]
-    else:
-        out_hbm = refs[0]
-        refs = refs[1:]
-    (wo, wg, wu, wd, att, x, norm, h, act, sd, sx, sg, rd, rx, ra,
-     wsem, isem, sd_sem, sx_sem, sg_sem, rd_sem, rx_sem, ra_sem, *refs) = refs
+GC = 4
+SLOT = 8
+
+
+def mega_kernel(pos_hbm, table_hbm, att_hbm, x_hbm, mnorm_hbm, anorm_hbm, wo_hbm, wg_hbm, wu_hbm, wd_hbm, wq_hbm, wk_hbm, wv_hbm, k_hbm, v_hbm,
+                out_hbm, new_hbm,
+                pos_ref, table, cs, wo, wg, wu, wd, wqkv, att, x, mnorm, anorm, h, act, qkv, q_rows, k_rows, v_rows, o_rows, new,
+                own, sd, sx, rd, rx,
+                wosem, gsem, usem, wsem, isem, sd_sem, sx_sem, sg_sem, rd_sem, rx_sem, ra_sem, osem):
     dim = x.shape[1]
     nch = dim // 2 // CW
+    ncol = wg.shape[0]
+    qcols = wq_hbm.shape[2]
+    kcols = wk_hbm.shape[2]
+    heads = qcols // 128
     tp = lax.axis_index("tp")
     core = lax.rem(tp, 2)
     sib = tp + 1 - 2 * core
@@ -255,26 +363,44 @@
     mine = pl.multiple_of(core * (dim // 2), CW)
     theirs = pl.multiple_of((1 - core) * (dim // 2), CW)
 
-    half_rows = wo.shape[0] // 2
+    def chunk(side, k):
+        return pl.ds(pl.multiple_of((theirs, mine)[side] + k * CW, CW), CW)
+
+    def wo_copy(layer, side, k):
+        return pltpu.make_async_copy(wo_hbm.at[layer, :, chunk(side, k)], wo.at[:, chunk(side, k)], wosem.at[side, k])
+
+    def gu_copies(layer, c):
+        cols = pl.ds(pl.multiple_of(c * 128, 128), 128)
+        return (pltpu.make_async_copy(wg_hbm.at[layer, :, cols], wg.at[c], gsem.at[c]),
+                pltpu.make_async_copy(wu_hbm.at[layer, :, cols], wu.at[c], usem.at[c]))
+
+    def kv_copies(half, c):
+        src = pl.ds(pl.multiple_of((half * HALF + c * SLOT) * 256, 2048), SLOT * 256)
+        dst = pl.ds(0, SLOT * 256)
+        return (pltpu.make_async_copy(k_hbm.at[1, src], wg.at[c, dst], gsem.at[c]),
+                pltpu.make_async_copy(v_hbm.at[1, src], wu.at[c, dst], usem.at[c]))
+
+    def wd_copy(layer):
+        return pltpu.make_async_copy(wd_hbm.at[layer], wd, wsem.at[0])
+
     att_copy = pltpu.make_async_copy(att_hbm, att, isem.at[0])
-    wo_copies = [pltpu.make_async_copy(wo_hbm.at[layer, pl.ds(r * half_rows, half_rows)], wo.at[pl.ds(r * half_rows, half_rows)], wsem.at[r]) for r in range(2)]
     x_copy = pltpu.make_async_copy(x_hbm, x, isem.at[1])
-    norm_copy = pltpu.make_async_copy(norm_hbm, norm, isem.at[2])
-    wg_copy = pltpu.make_async_copy(wg_hbm.at[layer], wg, wsem.at[2])
-    wu_copy = pltpu.make_async_copy(wu_hbm.at[layer], wu, wsem.at[3])
-    wd_copy = pltpu.make_async_copy(wd_hbm.at[layer], wd, wsem.at[4])
-    for c in [att_copy, *wo_copies]:
+    small = [pltpu.make_async_copy(mnorm_hbm, mnorm, isem.at[2]), pltpu.make_async_copy(anorm_hbm, anorm, isem.at[3]),
+             pltpu.make_async_copy(pos_hbm, pos_ref, isem.at[4]), pltpu.make_async_copy(table_hbm, table, isem.at[5])]
+    qkv_loads = [
+        pltpu.make_async_copy(wq_hbm.at[1], wqkv.at[:, pl.ds(0, qcols)], wsem.at[1]),
+        pltpu.make_async_copy(wk_hbm.at[1], wqkv.at[:, pl.ds(qcols, kcols)], wsem.at[2]),
+        pltpu.make_async_copy(wv_hbm.at[1], wqkv.at[:, pl.ds(qcols + kcols, kcols)], wsem.at[3]),
+    ]
+    att_copy.start()
+    wo_copy(0, 0, 0).start()
+    wo_copy(0, 1, 0).start()
+    x_copy.start()
+    for k in range(1, nch):
+        wo_copy(0, 0, k).start()
+        wo_copy(0, 1, k).start()
+    for c in small:
         c.start()
-    if next_qkv:
-        norm2, wqkv, qkv = refs
-        qcols = wq_hbm.shape[2]
-        kcols = wk_hbm.shape[2]
-        qkv_loads = [
-            pltpu.make_async_copy(norm2_hbm, norm2, isem.at[3]),
-            pltpu.make_async_copy(wq_hbm.at[layer + 1], wqkv.at[:, pl.ds(0, qcols)], wsem.at[5]),
-            pltpu.make_async_copy(wk_hbm.at[layer + 1], wqkv.at[:, pl.ds(qcols, kcols)], wsem.at[6]),
-            pltpu.make_async_copy(wv_hbm.at[layer + 1], wqkv.at[:, pl.ds(qcols + kcols, kcols)], wsem.at[7]),
-        ]
 
     barrier = pltpu.get_barrier_semaphore()
     for other in (sib, peer):
@@ -282,26 +408,44 @@
     pl.semaphore_wait(barrier, 2)
 
     def to_sib(ph, k):
-        return pltpu.make_async_remote_copy(sd.at[ph % 2, k], rd.at[ph, k], sd_sem.at[ph, k], rd_sem.at[ph, k],
+        return pltpu.make_async_remote_copy(sd.at[ph % 2, k], rd.at[ph % 4, k], sd_sem.at[ph, k], rd_sem.at[ph, k],
                                             device_id={"tp": sib}, device_id_type=MESH)
 
     def to_peer(ph, k):
-        return pltpu.make_async_remote_copy(sx.at[ph % 2, k], rx.at[ph, k], sx_sem.at[ph, k], rx_sem.at[ph, k],
+        return pltpu.make_async_remote_copy(sx.at[ph % 2, k], rx.at[ph % 4, k], sx_sem.at[ph, k], rx_sem.at[ph, k],
                                             device_id={"tp": peer}, device_id_type=MESH)
 
+    def final(ph):
+        return ph >= 6
+
     def share(ph, k):
-        return pltpu.make_async_remote_copy(sg.at[ph % 2, k], ra.at[ph, k], sg_sem.at[ph, k], ra_sem.at[ph, k],
+        rows = pl.ds((ph % 2) * HALF, HALF)
+        dst = out_hbm if final(ph) else x
+        return pltpu.make_async_remote_copy(x.at[rows, chunk(1, k)], dst.at[rows, chunk(1, k)], sg_sem.at[ph, k], ra_sem.at[ph, k],
                                             device_id={"tp": sib}, device_id_type=MESH)
 
-    def reduce_start(ph, lhs, w_ref):
+    def keep(ph, k):
+        rows = pl.ds((ph % 2) * HALF, HALF)
+        return pltpu.make_async_copy(x.at[rows, chunk(1, k)], out_hbm.at[rows, chunk(1, k)], osem.at[ph % 2, k])
+
+    def reduce_start(ph, lhs, w_ref, load):
+        def dot(side, k):
+            if load is not None:
+                load(side, k).wait()
+            return jnp.dot(lhs, w_ref[:, chunk(side, k)], preferred_element_type=F32)
+
+        def forward(k):
+            to_sib(ph, k).wait_recv()
+            sx[ph % 2, k] = (own[k] + rd[ph % 4, k].astype(F32)).astype(BF)
+            to_peer(ph, k).start()
+
         for k in range(nch):
-            sd[ph % 2, k] = jnp.dot(lhs, w_ref[:, pl.ds(theirs + k * CW, CW)], preferred_element_type=F32).astype(BF)
+            sd[ph % 2, k] = dot(0, k).astype(BF)
             to_sib(ph, k).start()
-        for k in range(nch):
-            part = jnp.dot(lhs, w_ref[:, pl.ds(mine + k * CW, CW)], preferred_element_type=F32)
-            to_sib(ph, k).wait_recv()
-            sx[ph % 2, k] = (part + rd[ph, k].astype(F32)).astype(BF)
-            to_peer(ph, k).start()
+            if k > 0:
+                forward(k - 1)
+            own[k] = dot(1, k)
+        forward(nch - 1)
         for k in range(nch):
             to_sib(ph, k).wait_send()
 
@@ -309,108 +453,209 @@
         rows = pl.ds((ph % 2) * HALF, HALF)
         for k in range(nch):
             to_peer(ph, k).wait()
-            total = (sx[ph % 2, k].astype(F32) + rx[ph, k].astype(F32)).astype(BF)
-            sg[ph % 2, k] = total
+            total = (sx[ph % 2, k].astype(F32) + rx[ph % 4, k].astype(F32)).astype(BF)
+            x[rows, chunk(1, k)] = (x[rows, chunk(1, k)].astype(F32) + total.astype(F32)).astype(BF)
             share(ph, k).start()
-            cols = pl.ds(mine + k * CW, CW)
-            x[rows, cols] = (x[rows, cols].astype(F32) + total.astype(F32)).astype(BF)
+            if final(ph):
+                keep(ph, k).start()
         for k in range(nch):
             share(ph, k).wait()
-            cols = pl.ds(theirs + k * CW, CW)
-            x[rows, cols] = (x[rows, cols].astype(F32) + ra[ph, k].astype(F32)).astype(BF)
-
-    def mlp(half):
+
+    def gate_up(layer, half):
         rows = pl.ds(half * HALF, HALF)
-        h[...] = normed(x[rows, :].astype(F32), norm[layer:layer + 1, :].astype(F32))
-
-        @pl.loop(0, act.shape[1] // GW)
+        h[...] = normed(x[rows, :].astype(F32), mnorm[layer:layer + 1, :].astype(F32))
+
+        @pl.loop(0, ncol // GC)
         def _(n):
-            cols = pl.ds(pl.multiple_of(n * GW, GW), GW)
-            g = jnp.dot(h[...], wg[:, cols], preferred_element_type=F32).astype(BF).astype(F32)
-            u = jnp.dot(h[...], wu[:, cols], preferred_element_type=F32).astype(BF).astype(F32)
+            if half == 0:
+                for c in range(GC):
+                    for cp in gu_copies(layer, n * GC + c):
+                        cp.wait()
+            wide = lambda ref: jnp.concatenate([ref[n * GC + c] for c in range(GC)], axis=1)
+            g = jnp.dot(h[...], wide(wg), preferred_element_type=F32).astype(BF).astype(F32)
+            u = jnp.dot(h[...], wide(wu), preferred_element_type=F32).astype(BF).astype(F32)
+            cols = pl.ds(pl.multiple_of(n * GC * 128, GC * 128), GC * 128)
             act[:, cols] = (g * jax.nn.sigmoid(g) * u).astype(BF)
 
-    def out_copy(half):
+    def qkv_rope(half):
         rows = pl.ds(half * HALF, HALF)
-        return pltpu.make_async_copy(x.at[rows], out_hbm.at[rows], isem.at[4 + half])
-
-    def qkv_copy(half):
+        h[...] = normed(x[rows, :].astype(F32), anorm[1:2, :].astype(F32))
+
+        @pl.loop(0, qkv.shape[0])
+        def _(n):
+            cols = pl.ds(pl.multiple_of(n * 256, 256), 256)
+            qkv[n] = jnp.dot(h[...], wqkv[:, cols], preferred_element_type=F32).astype(BF)
+
+        cos_b = cs[rows, 0:128]
+        sin_b = cs[rows, 128:256]
+
+        def piece(n, i):
+            return qkv[n, :, i * 128:i * 128 + 128].astype(F32)
+
+        def rope(vec):
+            return (vec * cos_b + pltpu.roll(vec, 64, 1) * sin_b).astype(BF)
+
+        k_new = [rope(piece(heads // 2, i)) for i in range(2)]
+        v_new = [piece(heads // 2 + 1, i) for i in range(2)]
+        for i in range(2):
+            new[i, rows, :] = k_new[i]
+            new[2 + i, rows, :] = v_new[i].astype(BF)
+        zero = jnp.zeros((HALF, 128), F32)
+        for j in range(8):
+            out_rows = pl.ds(j, HALF, stride=8)
+            kv = 0 if j < heads // 2 else 1
+            q_rows[out_rows, :] = rope(piece(j // 2, j % 2)).astype(F32) if j < heads else zero
+            k_rows[out_rows, :] = k_new[kv].astype(F32)
+            v_rows[out_rows, :] = v_new[kv]
+
+    col = lax.broadcasted_iota(jnp.int32, (8, 256), 1)
+    row = lax.broadcasted_iota(jnp.int32, (8, 256), 0)
+    key_row = jnp.where((col & 1) == jnp.where(row >= heads // 2, 1, 0), col >> 1, 4096)
+    scale = 128 ** -0.5
+
+    def attend(half):
+        @pl.loop(0, ncol // 2)
+        def _(i):
+            for c in range(2):
+                for cp in kv_copies(half, 2 * i + c):
+                    cp.wait()
+            pairs = range(SLOT)
+            zero8 = jnp.zeros((8, 128), F32)
+
+            def rows8(p, b):
+                return pl.ds(pl.multiple_of((i * 2 * SLOT + 2 * p + b) * 8, 8), 8)
+
+            def pos(p, b):
+                return pos_ref[half * HALF + i * 2 * SLOT + 2 * p + b]
+
+            def both(ref, p):
+                r = 2 * p % SLOT
+                slot = 2 * i + 2 * p // SLOT
+                return jnp.concatenate([ref[slot, r * 256:(r + 1) * 256, :], ref[slot, (r + 1) * 256:(r + 2) * 256, :]], axis=1)
+
+            scores, fresh = [], []
+            for p in pairs:
+                qa = q_rows[rows8(p, 0), :]
+                qb = q_rows[rows8(p, 1), :]
+                q2 = jnp.concatenate([jnp.concatenate([qa, zero8], axis=1), jnp.concatenate([zero8, qb], axis=1)], axis=0).astype(BF)
+                scores.append(lax.dot_general(q2, both(wg, p), (((1,), (1,)), ((), ())), preferred_element_type=F32))
+                prod = jnp.concatenate([qa * k_rows[rows8(p, 0), :], qb * k_rows[rows8(p, 1), :]], axis=0)
+                fresh.append(jnp.sum(prod, axis=-1, keepdims=True) * scale)
+            weights, last = [], []
+            for p in pairs:
+                before = jnp.concatenate([key_row < pos(p, 0), key_row < pos(p, 1)], axis=0)
+                s = jnp.where(before, scores[p] * scale, NEG)
+                peak = jnp.maximum(jnp.max(s, axis=-1, keepdims=True), fresh[p])
+                e = jnp.exp(s - peak)
+                e_new = jnp.exp(fresh[p] - peak)
+                inv = 1.0 / (jnp.sum(e, axis=-1, keepdims=True) + e_new)
+                weights.append((e * inv).astype(BF))
+                last.append((e_new * inv).astype(BF).astype(F32))
+            outs = [jnp.dot(weights[p], both(wu, p), preferred_element_type=F32) for p in pairs]
+            for p in pairs:
+                o_rows[rows8(p, 0), :] = outs[p][0:8, 0:128] + last[p][0:8] * v_rows[rows8(p, 0), :]
+                o_rows[rows8(p, 1), :] = outs[p][8:16, 128:256] + last[p][8:16] * v_rows[rows8(p, 1), :]
+            for c in range(2):
+                for cp in (kv_copies(1, 2 * i + c) if half == 0 else gu_copies(1, 2 * i + c)):
+                    cp.start()
+
         rows = pl.ds(half * HALF, HALF)
-        return pltpu.make_async_copy(qkv.at[:, rows], qkv_hbm.at[:, rows], isem.at[6 + half])
+        for j in range(heads):
+            att[rows, j * 128:(j + 1) * 128] = o_rows[pl.ds(j, HALF, stride=8), :].astype(BF)
+
+    def att_half(half):
+        return att[half * HALF:(half + 1) * HALF, :]
 
     att_copy.wait()
-    for c in wo_copies:
+    x_copy.wait()
+    reduce_start(0, att_half(0), wo, lambda side, k: wo_copy(0, side, k))
+
+    @pl.loop(0, ncol)
+    def _(c):
+        for cp in gu_copies(0, c):
+            cp.start()
+
+    wd_copy(0).start()
+    for c in qkv_loads:
+        c.start()
+    reduce_start(1, att_half(1), wo, None)
+    for k in range(nch):
+        wo_copy(1, 0, k).start()
+        wo_copy(1, 1, k).start()
+    for c in small:
         c.wait()
-    for c in (x_copy, norm_copy, wg_copy, wu_copy):
-        c.start()
-    for half in range(2):
-        reduce_start(half, att[half * HALF:(half + 1) * HALF, :], wo)
-    wd_copy.start()
-    if next_qkv:
-        for c in qkv_loads:
-            c.start()
-    x_copy.wait()
-    norm_copy.wait()
+
+    @pl.loop(0, 2 * HALF // 8)
+    def _(i):
+        for b in range(8):
+            r = i * 8 + b
+            cs[pl.ds(r, 1), :] = table[pl.ds(pos_ref[r], 1), :]
+
     for half in range(2):
         reduce_end(half)
+        gate_up(0, half)
         if half == 0:
-            wg_copy.wait()
-            wu_copy.wait()
-        mlp(half)
+            wd_copy(0).wait()
+        else:
+            @pl.loop(0, ncol)
+            def _(c):
+                for cp in kv_copies(0, c):
+                    cp.start()
+
+        reduce_start(2 + half, act[...], wd, None)
+    wd_copy(1).start()
+    for c in qkv_loads:
+        c.wait()
+    for half in range(2):
+        reduce_end(2 + half)
+        qkv_rope(half)
+        attend(half)
+        reduce_start(4 + half, att_half(half), wo, (lambda side, k: wo_copy(1, side, k)) if half == 0 else None)
+    new_copy = pltpu.make_async_copy(new, new_hbm, isem.at[6])
+    new_copy.start()
+    for half in range(2):
+        reduce_end(4 + half)
+        gate_up(1, half)
         if half == 0:
-            wd_copy.wait()
-        reduce_start(2 + half, act[...], wd)
-    if next_qkv:
-        for c in qkv_loads:
-            c.wait()
+            wd_copy(1).wait()
+        reduce_start(6 + half, act[...], wd, None)
     for half in range(2):
-        rows = pl.ds(half * HALF, HALF)
-        reduce_end(2 + half)
-        out_copy(half).start()
-        if next_qkv:
-            h[...] = normed(x[rows, :].astype(F32), norm2[layer + 1:layer + 2, :].astype(F32))
-
-            @pl.loop(0, qkv.shape[0])
-            def _(n):
-                cols = pl.ds(pl.multiple_of(n * 256, 256), 256)
-                qkv[n, rows, :] = jnp.dot(h[...], wqkv[:, cols], preferred_element_type=F32).astype(BF)
-
-            qkv_copy(half).start()
+        reduce_end(6 + half)
+    new_copy.wait()
     for half in range(2):
-        out_copy(half).wait()
-        if next_qkv:
-            qkv_copy(half).wait()
-
-
-def mlp_block(layer, att, hidden, norm, wo, wg, wu, wd, following):
+        for k in range(nch):
+            keep(6 + half, k).wait()
+
+
+def mega(positions, table, att, hidden, mnorm, anorm, wo, wg, wu, wd, wq, wk, wv, k_rows, v_rows):
     batch, dim = hidden.shape
     nch = dim // 2 // CW
+    cols = wq.shape[2] + 2 * wk.shape[2]
+    ncol = wg.shape[2] // 128
     anyspec = pl.BlockSpec(memory_space=pl.ANY)
     msg = lambda n: pltpu.VMEM((n, nch, HALF, CW), BF)
-    sems = pltpu.SemaphoreType.DMA((4, nch))
-    args = [att, hidden, norm, wo, wg, wu, wd]
-    scratch = [
-        pltpu.VMEM(wo.shape[1:], BF), pltpu.VMEM(wg.shape[1:], BF), pltpu.VMEM(wu.shape[1:], BF), pltpu.VMEM(wd.shape[1:], BF),
-        pltpu.VMEM(att.shape, BF), pltpu.VMEM(hidden.shape, BF), pltpu.VMEM(norm.shape, BF),
-        pltpu.VMEM((HALF, dim), BF), pltpu.VMEM((HALF, wd.shape[1]), BF),
-        msg(2), msg(2), msg(2), msg(4), msg(4), msg(4),
-        pltpu.SemaphoreType.DMA((8,)), pltpu.SemaphoreType.DMA((8,)), sems, sems, sems, sems, sems, sems,
-    ]
-    out_shape = [jax.ShapeDtypeStruct((batch, dim), BF)]
-    if following is not None:
-        norm2, wq, wk, wv = following
-        args += list(following)
-        cols = wq.shape[2] + 2 * wk.shape[2]
-        out_shape.append(jax.ShapeDtypeStruct((cols // 256, batch, 256), BF))
-        scratch += [pltpu.VMEM(norm2.shape, BF), pltpu.VMEM((dim, cols), BF), pltpu.VMEM((cols // 256, batch, 256), BF)]
+    sems = pltpu.SemaphoreType.DMA((8, nch))
+    rows = pltpu.VMEM((HALF * 8, 128), F32)
+    args = [positions, table, att, hidden, mnorm, anorm, wo, wg, wu, wd, wq, wk, wv, k_rows, v_rows]
     return pl.pallas_call(
-        functools.partial(mlp_kernel, layer, following is not None),
-        out_shape=out_shape,
+        mega_kernel,
+        out_shape=(jax.ShapeDtypeStruct((batch, dim), BF), jax.ShapeDtypeStruct((4, batch, 128), BF)),
         in_specs=[anyspec] * len(args),
-        out_specs=[anyspec] * len(out_shape),
-        scratch_shapes=scratch,
-        compiler_params=pltpu.CompilerParams(collective_id=layer, has_side_effects=True, vmem_limit_bytes=67043328),
-        name=f"mlp{layer}",
+        out_specs=(anyspec, anyspec),
+        scratch_shapes=[
+            pltpu.SMEM((batch,), jnp.int32), pltpu.VMEM(table.shape, F32), pltpu.VMEM((batch, table.shape[1]), F32),
+            pltpu.VMEM(wo.shape[1:], BF), pltpu.VMEM((ncol, dim, 128), BF), pltpu.VMEM((ncol, dim, 128), BF), pltpu.VMEM(wd.shape[1:], BF),
+            pltpu.VMEM((dim, cols), BF), pltpu.VMEM(att.shape, BF), pltpu.VMEM(hidden.shape, BF),
+            pltpu.VMEM(mnorm.shape, BF), pltpu.VMEM(anorm.shape, BF),
+            pltpu.VMEM((HALF, dim), BF), pltpu.VMEM((HALF, wd.shape[1]), BF), pltpu.VMEM((cols // 256, HALF, 256), BF),
+            rows, rows, rows, rows, pltpu.VMEM((4, batch, 128), BF),
+            pltpu.VMEM((nch, HALF, CW), F32), msg(2), msg(2), msg(4), msg(4),
+            pltpu.SemaphoreType.DMA((2, nch)), pltpu.SemaphoreType.DMA((ncol,)), pltpu.SemaphoreType.DMA((ncol,)),
+            pltpu.SemaphoreType.DMA((4,)), pltpu.SemaphoreType.DMA((7,)),
+            sems, sems, sems, sems, sems, sems, pltpu.SemaphoreType.DMA((2, nch)),
+        ],
+        compiler_params=pltpu.CompilerParams(collective_id=0, has_side_effects=True, vmem_limit_bytes=67043328),
+        name="mega",
     )(*args)
 
 
@@ -427,13 +672,12 @@
         flat = (cache_shape[0], cache_shape[1], cache_shape[2] * cache_shape[3], cache_shape[4])
         k_flat, v_flat = k_cache.reshape(flat), v_cache.reshape(flat)
         table = jnp.asarray(rope_table(cache_shape[2], cache_shape[4]))
-        layers = cache_shape[0]
-        caches = None
         source = (hidden, attn_norm, w_query, w_key, w_value)
-        for layer in range(layers):
-            att, *caches = attention(layer, positions, table, source, k_flat, v_flat, caches, w_query.shape[2], w_key.shape[2])
-            following = (attn_norm, w_query, w_key, w_value) if layer + 1 < layers else None
-            hidden, *source = mlp_block(layer, att, hidden, mlp_norm, w_out, w_gate, w_up, w_down, following)
+        att, *caches = attention(0, positions, table, source, k_flat, v_flat, None, w_query.shape[2], w_key.shape[2])
+        rows = (cache_shape[0], -1, cache_shape[4])
+        hidden, new = mega(positions, table, att, hidden, mlp_norm, attn_norm, w_out, w_gate, w_up, w_down, w_query, w_key, w_value,
+                           k_cache.reshape(rows), v_cache.reshape(rows))
+        caches = write_rows(1, positions, new, k_flat, v_flat, caches)
         return hidden, caches[0].reshape(cache_shape), caches[1].reshape(cache_shape)
 
     return jax.shard_map(local_step, mesh=mesh, in_specs=(row_spec, pos_spec, cache_spec, cache_spec, norm_spec, col_spec, col_spec, col_spec, split_rows, norm_spec, col_spec, col_spec, split_rows), out_specs=(row_spec, cache_spec, cache_spec), check_vma=False)

time: 147 us -> 139 us (0.946)
  Pallas kernels: 143 us -> 135 us
    pallas_call x2 -> x1, Pallas kernels: 49.2 us -> 23.6 us  [attention(): pl.pallas_call(functools.partial(attn_kernel, layer, has_qkv, prev is not...]
    pallas_call x2, Pallas kernels: 93.9 us -> 112 us  [the longest x1 90.5 us: mega(): pl.pallas_call(mega_kernel, out_shape=(jax.ShapeDtypeStruct((batch, dim),...]
where the time goes in v3:
time: 139 us; the launch traced here: 138 us
  Pallas kernels  135 us (97%)
  local copies, waits for them, and re-layouts  2.65 us (2%)
    pallas_call x1, Pallas kernels, mega(): pl.pallas_call(mega_kernel, out_shape=(jax.ShapeDtypeStruct((batch, dim),...  90.5 us
    pallas_call x1, Pallas kernels, attention(): pl.pallas_call(functools.partial(attn_kernel, layer, has_qkv, prev is not...  23.6 us
    pallas_call x1, Pallas kernels, write_rows(): pl.pallas_call(functools.partial(write_kernel, layer), out_shape=(jax.Sha...  21.1 us

profile of v3, /device:TPU:0, one launch (start us, length us, event | category | flops | bytes accessed | tf_op | source)
XLA Modules:
  0.0 138.5 jit_solution(16321831500383600651)
XLA Ops:
  0.6 23.6 %attn0.1 = (bf16[256,768]{1,0:T(8,128)(2,1)}, bf16[2,256,256,128]{3,2,1,0:T(8,128)(2,1)}, bf16[2,256,256,128]{3,2,1,0:T(8,128)(2,1)}) custom-call(s32[256]{0:T(256)} %pos_hbm.3, f32[128,256]{1,0:T(8,128)} %constant.2.clone.refs_1_.table_hbm, bf16[256,3072]{1,0:T(8,128)(2,1)} %x_hbm.1, bf16[2,3072]{1,0:T(2,128)(2,1)} %anorm_hbm.1, ...), custom_call_target="tpu_custom_call" | custom-call | flops 2013265920 | bytes 79691776 | tf_op jit(solution)/shard_map/attn0/pallas_call | solution.py:233
  24.3 90.5 %mega.1 = (bf16[256,3072]{1,0:T(8,128)(2,1)}, bf16[4,256,128]{2,1,0:T(8,128)(2,1)}) custom-call(s32[256]{0:T(256)} %pos_hbm.3, f32[128,256]{1,0:T(8,128)} %constant.2.clone.refs_1_.table_hbm, bf16[256,768]{1,0:T(8,128)(2,1)} %get-tuple-element.10.att_hbm, bf16[256,3072]{1,0:T(8,128)(2,1)} %x_hbm.1, bf16[2,3072]{1,0:T(2,128)(2,1)} %mnorm_hbm.1, ...), custom_call_target="tpu_custom_call" | custom-call | tf_op jit(solution)/shard_map/mega/pallas_call | solution.py:640
  114.8 21.1 %write_rows.1 = (bf16[2,256,256,128]{3,2,1,0:T(8,128)(2,1)}, bf16[2,256,256,128]{3,2,1,0:T(8,128)(2,1)}) custom-call(s32[256]{0:T(256)} %pos_hbm.3, bf16[4,256,128]{2,1,0:T(8,128)(2,1)} %get-tuple-element.12.new_hbm, bf16[2,256,256,128]{3,2,1,0:T(8,128)(2,1)} %bitcast.8, ...), custom_call_target="tpu_custom_call", output_to_operand_aliasing={{0}: (4, {}), {1}: (5, {})} | custom-call | bytes 70254592 | tf_op jit(solution)/shard_map/write_rows/pallas_call | solution.py:319
  135.8 2.7 %copy.22 = bf16[256,3072]{1,0:T(8,128)(2,1)} copy(bf16[256,3072]{1,0:T(8,128)(2,1)} %get-tuple-element.20) | data formatting | bytes 3145728

commit v4 on v3

--- a/solution.py
+++ b/solution.py
@@ -347,7 +347,7 @@
 
 def mega_kernel(pos_hbm, table_hbm, att_hbm, x_hbm, mnorm_hbm, anorm_hbm, wo_hbm, wg_hbm, wu_hbm, wd_hbm, wq_hbm, wk_hbm, wv_hbm, k_hbm, v_hbm,
                 out_hbm, new_hbm,
-                pos_ref, table, cs, wo, wg, wu, wd, wqkv, att, x, mnorm, anorm, h, act, qkv, q_rows, k_rows, v_rows, o_rows, new,
+                pos_ref, table, cs, wo, wg, wu, wd, wqkv, att, x, mnorm, anorm, h, act, qkv, q_rows, k_rows, v_rows, o_rows, s_buf, new,
                 own, sd, sx, rd, rx,
                 wosem, gsem, usem, wsem, isem, sd_sem, sx_sem, sg_sem, rd_sem, rx_sem, ra_sem, osem):
     dim = x.shape[1]
@@ -432,24 +432,37 @@
         def dot(side, k):
             if load is not None:
                 load(side, k).wait()
-            return jnp.dot(lhs, w_ref[:, chunk(side, k)], preferred_element_type=F32)
+            return jnp.dot(lhs(), w_ref[:, chunk(side, k)], preferred_element_type=F32)
+
+        def send(k):
+            sd[ph % 2, k] = dot(0, k).astype(BF)
+            to_sib(ph, k).start()
+
+        def hold(k):
+            own[k] = dot(1, k)
 
         def forward(k):
             to_sib(ph, k).wait_recv()
             sx[ph % 2, k] = (own[k] + rd[ph % 4, k].astype(F32)).astype(BF)
             to_peer(ph, k).start()
 
-        for k in range(nch):
-            sd[ph % 2, k] = dot(0, k).astype(BF)
-            to_sib(ph, k).start()
-            if k > 0:
-                forward(k - 1)
-            own[k] = dot(1, k)
-        forward(nch - 1)
-        for k in range(nch):
-            to_sib(ph, k).wait_send()
-
-    def reduce_end(ph):
+        send(0)
+        send(1)
+        hold(0)
+        for k in range(2, nch):
+            send(k)
+        forward(0)
+
+        def rest():
+            for k in range(1, nch):
+                hold(k)
+                forward(k)
+            for k in range(nch):
+                to_sib(ph, k).wait_send()
+
+        return rest
+
+    def reduce_end(ph, between=None):
         rows = pl.ds((ph % 2) * HALF, HALF)
         for k in range(nch):
             to_peer(ph, k).wait()
@@ -458,6 +471,8 @@
             share(ph, k).start()
             if final(ph):
                 keep(ph, k).start()
+        if between is not None:
+            between()
         for k in range(nch):
             share(ph, k).wait()
 
@@ -481,10 +496,9 @@
         rows = pl.ds(half * HALF, HALF)
         h[...] = normed(x[rows, :].astype(F32), anorm[1:2, :].astype(F32))
 
-        @pl.loop(0, qkv.shape[0])
-        def _(n):
-            cols = pl.ds(pl.multiple_of(n * 256, 256), 256)
-            qkv[n] = jnp.dot(h[...], wqkv[:, cols], preferred_element_type=F32).astype(BF)
+        full = jnp.dot(h[...], wqkv[...], preferred_element_type=F32).astype(BF)
+        for n in range(qkv.shape[0]):
+            qkv[n] = full[:, n * 256:(n + 1) * 256]
 
         cos_b = cs[rows, 0:128]
         sin_b = cs[rows, 128:256]
@@ -514,61 +528,75 @@
     scale = 128 ** -0.5
 
     def attend(half):
-        @pl.loop(0, ncol // 2)
-        def _(i):
+        pairs = range(SLOT)
+        zero8 = jnp.zeros((8, 128), F32)
+        steps = ncol // 2
+
+        def rows8(i, p, b):
+            return pl.ds(pl.multiple_of((i * 2 * SLOT + 2 * p + b) * 8, 8), 8)
+
+        def both(ref, i, p):
+            r = 2 * p % SLOT
+            slot = 2 * i + 2 * p // SLOT
+            return jnp.concatenate([ref[slot, r * 256:(r + 1) * 256, :], ref[slot, (r + 1) * 256:(r + 2) * 256, :]], axis=1)
+
+        def score(i):
+            for p in pairs:
+                qa = q_rows[rows8(i, p, 0), :]
+                qb = q_rows[rows8(i, p, 1), :]
+                q2 = jnp.concatenate([jnp.concatenate([qa, zero8], axis=1), jnp.concatenate([zero8, qb], axis=1)], axis=0).astype(BF)
+                s_buf[lax.rem(i, 2), p] = lax.dot_general(q2, both(wg, i, p), (((1,), (1,)), ((), ())), preferred_element_type=F32)
+
+        def step(i, more):
+            if more:
+                for c in range(2):
+                    kv_copies(half, 2 * i + 2 + c)[0].wait()
             for c in range(2):
-                for cp in kv_copies(half, 2 * i + c):
-                    cp.wait()
-            pairs = range(SLOT)
-            zero8 = jnp.zeros((8, 128), F32)
-
-            def rows8(p, b):
-                return pl.ds(pl.multiple_of((i * 2 * SLOT + 2 * p + b) * 8, 8), 8)
-
-            def pos(p, b):
-                return pos_ref[half * HALF + i * 2 * SLOT + 2 * p + b]
-
-            def both(ref, p):
-                r = 2 * p % SLOT
-                slot = 2 * i + 2 * p // SLOT
-                return jnp.concatenate([ref[slot, r * 256:(r + 1) * 256, :], ref[slot, (r + 1) * 256:(r + 2) * 256, :]], axis=1)
-
-            scores, fresh = [], []
-            for p in pairs:
-                qa = q_rows[rows8(p, 0), :]
-                qb = q_rows[rows8(p, 1), :]
-                q2 = jnp.concatenate([jnp.concatenate([qa, zero8], axis=1), jnp.concatenate([zero8, qb], axis=1)], axis=0).astype(BF)
-                scores.append(lax.dot_general(q2, both(wg, p), (((1,), (1,)), ((), ())), preferred_element_type=F32))
-                prod = jnp.concatenate([qa * k_rows[rows8(p, 0), :], qb * k_rows[rows8(p, 1), :]], axis=0)
-                fresh.append(jnp.sum(prod, axis=-1, keepdims=True) * scale)
+                kv_copies(half, 2 * i + c)[1].wait()
+            scores = [s_buf[lax.rem(i, 2), p] for p in pairs]
+            if more:
+                score(i + 1)
             weights, last = [], []
             for p in pairs:
-                before = jnp.concatenate([key_row < pos(p, 0), key_row < pos(p, 1)], axis=0)
+                prod = jnp.concatenate([q_rows[rows8(i, p, b), :] * k_rows[rows8(i, p, b), :] for b in range(2)], axis=0)
+                fresh = jnp.sum(prod, axis=-1, keepdims=True) * scale
+                pos = [pos_ref[half * HALF + i * 2 * SLOT + 2 * p + b] for b in range(2)]
+                before = jnp.concatenate([key_row < pos[0], key_row < pos[1]], axis=0)
                 s = jnp.where(before, scores[p] * scale, NEG)
-                peak = jnp.maximum(jnp.max(s, axis=-1, keepdims=True), fresh[p])
+                peak = jnp.maximum(jnp.max(s, axis=-1, keepdims=True), fresh)
                 e = jnp.exp(s - peak)
-                e_new = jnp.exp(fresh[p] - peak)
+                e_new = jnp.exp(fresh - peak)
                 inv = 1.0 / (jnp.sum(e, axis=-1, keepdims=True) + e_new)
                 weights.append((e * inv).astype(BF))
                 last.append((e_new * inv).astype(BF).astype(F32))
-            outs = [jnp.dot(weights[p], both(wu, p), preferred_element_type=F32) for p in pairs]
+            outs = [jnp.dot(weights[p], both(wu, i, p), preferred_element_type=F32) for p in pairs]
             for p in pairs:
-                o_rows[rows8(p, 0), :] = outs[p][0:8, 0:128] + last[p][0:8] * v_rows[rows8(p, 0), :]
-                o_rows[rows8(p, 1), :] = outs[p][8:16, 128:256] + last[p][8:16] * v_rows[rows8(p, 1), :]
+                o_rows[rows8(i, p, 0), :] = outs[p][0:8, 0:128] + last[p][0:8] * v_rows[rows8(i, p, 0), :]
+                o_rows[rows8(i, p, 1), :] = outs[p][8:16, 128:256] + last[p][8:16] * v_rows[rows8(i, p, 1), :]
             for c in range(2):
                 for cp in (kv_copies(1, 2 * i + c) if half == 0 else gu_copies(1, 2 * i + c)):
                     cp.start()
 
+        for c in range(2):
+            kv_copies(half, c)[0].wait()
+        score(0)
+
+        @pl.loop(0, steps - 1)
+        def _(i):
+            step(i, True)
+
+        step(steps - 1, False)
+
         rows = pl.ds(half * HALF, HALF)
         for j in range(heads):
             att[rows, j * 128:(j + 1) * 128] = o_rows[pl.ds(j, HALF, stride=8), :].astype(BF)
 
     def att_half(half):
-        return att[half * HALF:(half + 1) * HALF, :]
+        return lambda: att[half * HALF:(half + 1) * HALF, :]
 
     att_copy.wait()
     x_copy.wait()
-    reduce_start(0, att_half(0), wo, lambda side, k: wo_copy(0, side, k))
+    reduce_start(0, att_half(0), wo, lambda side, k: wo_copy(0, side, k))()
 
     @pl.loop(0, ncol)
     def _(c):
@@ -578,10 +606,7 @@
     wd_copy(0).start()
     for c in qkv_loads:
         c.start()
-    reduce_start(1, att_half(1), wo, None)
-    for k in range(nch):
-        wo_copy(1, 0, k).start()
-        wo_copy(1, 1, k).start()
+    rest = reduce_start(1, att_half(1), wo, None)
     for c in small:
         c.wait()
 
@@ -592,7 +617,11 @@
             cs[pl.ds(r, 1), :] = table[pl.ds(pos_ref[r], 1), :]
 
     for half in range(2):
-        reduce_end(half)
+        reduce_end(half, rest)
+        if half == 0:
+            for k in range(nch):
+                wo_copy(1, 0, k).start()
+                wo_copy(1, 1, k).start()
         gate_up(0, half)
         if half == 0:
             wd_copy(0).wait()
@@ -602,25 +631,26 @@
                 for cp in kv_copies(0, c):
                     cp.start()
 
-        reduce_start(2 + half, act[...], wd, None)
-    wd_copy(1).start()
-    for c in qkv_loads:
-        c.wait()
+        rest = reduce_start(2 + half, lambda: act[...], wd, None)
     for half in range(2):
-        reduce_end(2 + half)
+        reduce_end(2 + half, rest)
+        if half == 0:
+            wd_copy(1).start()
+            for c in qkv_loads:
+                c.wait()
         qkv_rope(half)
         attend(half)
-        reduce_start(4 + half, att_half(half), wo, (lambda side, k: wo_copy(1, side, k)) if half == 0 else None)
+        rest = reduce_start(4 + half, att_half(half), wo, (lambda side, k: wo_copy(1, side, k)) if half == 0 else None)
     new_copy = pltpu.make_async_copy(new, new_hbm, isem.at[6])
     new_copy.start()
     for half in range(2):
-        reduce_end(4 + half)
+        reduce_end(4 + half, rest)
         gate_up(1, half)
         if half == 0:
             wd_copy(1).wait()
-        reduce_start(6 + half, act[...], wd, None)
-    for half in range(2):
-        reduce_end(6 + half)
+        rest = reduce_start(6 + half, lambda: act[...], wd, None)
+    reduce_end(6, rest)
+    reduce_end(7)
     new_copy.wait()
     for half in range(2):
         for k in range(nch):
@@ -648,7 +678,7 @@
             pltpu.VMEM((dim, cols), BF), pltpu.VMEM(att.shape, BF), pltpu.VMEM(hidden.shape, BF),
             pltpu.VMEM(mnorm.shape, BF), pltpu.VMEM(anorm.shape, BF),
             pltpu.VMEM((HALF, dim), BF), pltpu.VMEM((HALF, wd.shape[1]), BF), pltpu.VMEM((cols // 256, HALF, 256), BF),
-            rows, rows, rows, rows, pltpu.VMEM((4, batch, 128), BF),
+            rows, rows, rows, rows, pltpu.VMEM((2, SLOT, 16, 256), F32), pltpu.VMEM((4, batch, 128), BF),
             pltpu.VMEM((nch, HALF, CW), F32), msg(2), msg(2), msg(4), msg(4),
             pltpu.SemaphoreType.DMA((2, nch)), pltpu.SemaphoreType.DMA((ncol,)), pltpu.SemaphoreType.DMA((ncol,)),
             pltpu.SemaphoreType.DMA((4,)), pltpu.SemaphoreType.DMA((7,)),

time: 139 us -> 131 us (0.942)
  Pallas kernels: 135 us -> 128 us
    pallas_call x1, Pallas kernels: 90.5 us -> 83.3 us  [mega(): pl.pallas_call(mega_kernel, out_shape=(jax.ShapeDtypeStruct((batch, dim),...]
where the time goes in v4:
time: 131 us
  Pallas kernels  128 us (98%)
  local copies, waits for them, and re-layouts  2.65 us (2%)
    pallas_call x1, Pallas kernels, mega(): pl.pallas_call(mega_kernel, out_shape=(jax.ShapeDtypeStruct((batch, dim),...  83.3 us
    pallas_call x1, Pallas kernels, attention(): pl.pallas_call(functools.partial(attn_kernel, layer, has_qkv, prev is not...  23.6 us
    pallas_call x1, Pallas kernels, write_rows(): pl.pallas_call(functools.partial(write_kernel, layer), out_shape=(jax.Sha...  21.1 us
    unnamed x1, local copies, waits for them, and re-layouts  2.65 us

profile of v4, /device:TPU:0, one launch (start us, length us, event | category | flops | bytes accessed | tf_op | source)
XLA Modules:
  0.0 131.3 jit_solution(2328094448641916725)
XLA Ops:
  0.6 23.6 %attn0.1 = (bf16[256,768]{1,0:T(8,128)(2,1)}, bf16[2,256,256,128]{3,2,1,0:T(8,128)(2,1)}, bf16[2,256,256,128]{3,2,1,0:T(8,128)(2,1)}) custom-call(s32[256]{0:T(256)} %pos_hbm.3, f32[128,256]{1,0:T(8,128)} %constant.2.clone.refs_1_.table_hbm, bf16[256,3072]{1,0:T(8,128)(2,1)} %x_hbm.1, bf16[2,3072]{1,0:T(2,128)(2,1)} %anorm_hbm.1, ...), custom_call_target="tpu_custom_call" | custom-call | flops 2013265920 | bytes 79691776 | tf_op jit(solution)/shard_map/attn0/pallas_call | solution.py:233
  24.3 83.3 %mega.1 = (bf16[256,3072]{1,0:T(8,128)(2,1)}, bf16[4,256,128]{2,1,0:T(8,128)(2,1)}) custom-call(s32[256]{0:T(256)} %pos_hbm.3, f32[128,256]{1,0:T(8,128)} %constant.2.clone.refs_1_.table_hbm, bf16[256,768]{1,0:T(8,128)(2,1)} %get-tuple-element.10.att_hbm, bf16[256,3072]{1,0:T(8,128)(2,1)} %x_hbm.1, bf16[2,3072]{1,0:T(2,128)(2,1)} %mnorm_hbm.1, ...), custom_call_target="tpu_custom_call" | custom-call | tf_op jit(solution)/shard_map/mega/pallas_call | solution.py:670
  107.6 21.1 %write_rows.1 = (bf16[2,256,256,128]{3,2,1,0:T(8,128)(2,1)}, bf16[2,256,256,128]{3,2,1,0:T(8,128)(2,1)}) custom-call(s32[256]{0:T(256)} %pos_hbm.3, bf16[4,256,128]{2,1,0:T(8,128)(2,1)} %get-tuple-element.12.new_hbm, bf16[2,256,256,128]{3,2,1,0:T(8,128)(2,1)} %bitcast.8, ...), custom_call_target="tpu_custom_call", output_to_operand_aliasing={{0}: (4, {}), {1}: (5, {})} | custom-call | bytes 70254592 | tf_op jit(solution)/shard_map/write_rows/pallas_call | solution.py:319
  128.6 2.7 %copy.22 = bf16[256,3072]{1,0:T(8,128)(2,1)} copy(bf16[256,3072]{1,0:T(8,128)(2,1)} %get-tuple-element.20) | data formatting | bytes 3145728

commit v5 on v4

--- a/solution.py
+++ b/solution.py
@@ -33,43 +33,38 @@
 
 
 BLK = 16
-HOLD = 4
-
-
-def attn_kernel(layer, has_qkv, aliased, *refs):
-    pos_hbm, table_hbm = refs[:2]
-    if has_qkv:
-        qkv_hbm, k_hbm, v_hbm = refs[2:5]
-        refs = refs[5:]
-    else:
-        x_hbm, norm_hbm, wq_hbm, wk_hbm, wv_hbm, k_hbm, v_hbm = refs[2:9]
-        refs = refs[9:]
-    if aliased:
-        refs = refs[2:]
-    att_hbm, ko_hbm, vo_hbm, pos_ref, table, qkv, cs, q_rows, k_rows, v_rows, o_rows, att, kbuf, vbuf, sem, insem, outsem, *rest = refs
+HOLD = 6
+
+
+def patch(kbuf, vbuf, k_rows, v_rows, pos_ref, i):
+    seq_in_group = lax.broadcasted_iota(jnp.int32, (16, 128), 0) >> 1
+    for b in range(BLK):
+        pos = pos_ref[i * BLK + b]
+        group = pl.ds(pl.multiple_of((pos >> 3) * 16, 16), 16)
+        hit = seq_in_group == (pos & 7)
+        rows = pl.ds(pl.multiple_of((i * BLK + b) * 8, 8), 8)
+        for buf, new in ((kbuf, k_rows), (vbuf, v_rows)):
+            new8 = new[rows, :]
+            new16 = jnp.concatenate([new8, new8], axis=0)
+            old16 = buf[i, b, group, :].astype(F32)
+            buf[i, b, group, :] = jnp.where(hit, new16, old16).astype(BF)
+
+
+def attn_kernel(layer, pos_hbm, table_hbm, x_hbm, norm_hbm, wq_hbm, wk_hbm, wv_hbm, k_hbm, v_hbm, att_hbm, ko_hbm, vo_hbm,
+                pos_ref, table, cs, q_rows, k_rows, v_rows, o_rows, s_buf, att, kbuf, vbuf, x_buf, norm, w_buf, h_buf, sem, insem, outsem):
     nblk = kbuf.shape[0]
     batch = nblk * BLK
     heads = att.shape[1] // 128
-
-    pos_copy = pltpu.make_async_copy(pos_hbm, pos_ref, sem.at[0])
-    table_copy = pltpu.make_async_copy(table_hbm, table, sem.at[1])
-    pos_copy.start()
-    table_copy.start()
-    if has_qkv:
-        first = [pltpu.make_async_copy(qkv_hbm, qkv, sem.at[2])]
-    else:
-        x_buf, norm, w_buf, h_buf = rest
-        qcols = wq_hbm.shape[2]
-        kcols = wk_hbm.shape[2]
-        x_copies = [pltpu.make_async_copy(x_hbm, x_buf, sem.at[3]), pltpu.make_async_copy(norm_hbm, norm, sem.at[4])]
-        for c in x_copies:
-            c.start()
-        first = [
-            pltpu.make_async_copy(wq_hbm.at[layer], w_buf.at[:, pl.ds(0, qcols)], sem.at[5]),
-            pltpu.make_async_copy(wk_hbm.at[layer], w_buf.at[:, pl.ds(qcols, kcols)], sem.at[6]),
-            pltpu.make_async_copy(wv_hbm.at[layer], w_buf.at[:, pl.ds(qcols + kcols, kcols)], sem.at[7]),
-        ]
-    for c in first:
+    qcols = wq_hbm.shape[2]
+    kcols = wk_hbm.shape[2]
+    first = [pltpu.make_async_copy(pos_hbm, pos_ref, sem.at[0]), pltpu.make_async_copy(table_hbm, table, sem.at[1])]
+    x_copies = [pltpu.make_async_copy(x_hbm, x_buf, sem.at[2]), pltpu.make_async_copy(norm_hbm, norm, sem.at[3])]
+    w_copies = [
+        pltpu.make_async_copy(wq_hbm.at[layer], w_buf.at[:, pl.ds(0, qcols)], sem.at[4]),
+        pltpu.make_async_copy(wk_hbm.at[layer], w_buf.at[:, pl.ds(qcols, kcols)], sem.at[5]),
+        pltpu.make_async_copy(wv_hbm.at[layer], w_buf.at[:, pl.ds(qcols + kcols, kcols)], sem.at[6]),
+    ]
+    for c in first + x_copies + w_copies:
         c.start()
 
     def in_copies(i):
@@ -87,8 +82,8 @@
         for c in in_copies(i):
             c.start()
 
-    pos_copy.wait()
-    table_copy.wait()
+    for c in first:
+        c.wait()
 
     @pl.loop(0, batch // 8)
     def _(i):
@@ -96,79 +91,69 @@
             r = i * 8 + b
             cs[pl.ds(r, 1), :] = table[pl.ds(pos_ref[r], 1), :]
 
-    if not has_qkv:
-        for c in x_copies:
-            c.wait()
-        h_buf[...] = normed(x_buf[...].astype(F32), norm[layer:layer + 1, :].astype(F32))
-    for c in first:
+    for c in x_copies:
         c.wait()
-    if not has_qkv:
-        @pl.loop(0, (qcols + 2 * kcols) // 256)
-        def _(n):
-            cols = pl.ds(pl.multiple_of(n * 256, 256), 256)
-            qkv[n] = jnp.dot(h_buf[...], w_buf[:, cols], preferred_element_type=F32).astype(BF)
-
+    h_buf[...] = normed(x_buf[...].astype(F32), norm[layer:layer + 1, :].astype(F32))
     cos_b = cs[:, 0:128]
     sin_b = cs[:, 128:256]
-
-    def piece(n, h):
-        return qkv[n, :, h * 128:h * 128 + 128].astype(F32)
+    for c in w_copies:
+        c.wait()
+    full = jnp.dot(h_buf[...], w_buf[...], preferred_element_type=F32).astype(BF)
+
+    def piece(j):
+        return full[:, j * 128:(j + 1) * 128].astype(F32)
 
     def rope(vec):
         return (vec * cos_b + pltpu.roll(vec, 64, 1) * sin_b).astype(BF).astype(F32)
 
     zero = jnp.zeros((batch, 128), F32)
     for j in range(8):
-        q_rows[pl.ds(j, batch, stride=8), :] = rope(piece(j // 2, j % 2)) if j < heads else zero
+        q_rows[pl.ds(j, batch, stride=8), :] = rope(piece(j)) if j < heads else zero
     for h in range(2):
-        k_vec = rope(piece(heads // 2, h))
-        v_vec = piece(heads // 2 + 1, h)
+        k_vec = rope(piece(heads + h))
+        v_vec = piece(heads + 2 + h)
         for r in range(4):
             k_rows[pl.ds(2 * r + h, batch, stride=8), :] = k_vec
             v_rows[pl.ds(2 * r + h, batch, stride=8), :] = v_vec
 
     col = lax.broadcasted_iota(jnp.int32, (8, 256), 1)
     row = lax.broadcasted_iota(jnp.int32, (8, 256), 0)
-    own = (col & 1) == jnp.where(row >= heads // 2, 1, 0)
-    key_row = jnp.where(own, col >> 1, 4096)
-    seq_in_group = lax.broadcasted_iota(jnp.int32, (16, 128), 0) >> 1
+    key_row = jnp.where((col & 1) == jnp.where(row >= heads // 2, 1, 0), col >> 1, 4096)
     scale = 128 ** -0.5
-
-    @pl.loop(0, nblk)
-    def _(i):
-        for c in in_copies(i):
-            c.wait()
-        for b in range(BLK):
-            pos = pos_ref[i * BLK + b]
-            group = pl.ds(pl.multiple_of((pos >> 3) * 16, 16), 16)
-            hit = seq_in_group == (pos & 7)
-            rows = pl.ds(pl.multiple_of((i * BLK + b) * 8, 8), 8)
-            for buf, new in ((kbuf, k_rows), (vbuf, v_rows)):
-                new8 = new[rows, :]
-                new16 = jnp.concatenate([new8, new8], axis=0)
-                old16 = buf[i, b, group, :].astype(F32)
-                buf[i, b, group, :] = jnp.where(hit, new16, old16).astype(BF)
-        zero8 = jnp.zeros((8, 128), F32)
-        pairs = range(BLK // 2)
-        scores = []
+    pairs = range(BLK // 2)
+    zero8 = jnp.zeros((8, 128), F32)
+
+    def both(buf, i, p):
+        return jnp.concatenate([buf[i, 2 * p], buf[i, 2 * p + 1]], axis=1)
+
+    def score(i):
         for p in pairs:
-            first = i * BLK + 2 * p
-            qa = q_rows[pl.ds(pl.multiple_of(first * 8, 8), 8), :]
-            qb = q_rows[pl.ds(pl.multiple_of(first * 8 + 8, 8), 8), :]
+            qa, qb = [q_rows[pl.ds(pl.multiple_of((i * BLK + 2 * p + b) * 8, 8), 8), :] for b in range(2)]
             q2 = jnp.concatenate([jnp.concatenate([qa, zero8], axis=1), jnp.concatenate([zero8, qb], axis=1)], axis=0).astype(BF)
-            k2 = jnp.concatenate([kbuf[i, 2 * p], kbuf[i, 2 * p + 1]], axis=1)
-            scores.append(lax.dot_general(q2, k2, (((1,), (1,)), ((), ())), preferred_element_type=F32))
+            s_buf[lax.rem(i, 2), p] = lax.dot_general(q2, both(kbuf, i, p), (((1,), (1,)), ((), ())), preferred_element_type=F32)
+
+    def step(i, more):
+        if more:
+            for c in in_copies(i + 1):
+                c.wait()
+            patch(kbuf, vbuf, k_rows, v_rows, pos_ref, i + 1)
+        scores = [s_buf[lax.rem(i, 2), p] for p in pairs]
+        if more:
+            score(i + 1)
         weights = []
         for p in pairs:
-            first = i * BLK + 2 * p
-            keep = jnp.concatenate([key_row <= pos_ref[first], key_row <= pos_ref[first + 1]], axis=0)
-            s = jnp.where(keep, scores[p] * scale, NEG)
+            first_row = i * BLK + 2 * p
+            seen = jnp.concatenate([key_row <= pos_ref[first_row], key_row <= pos_ref[first_row + 1]], axis=0)
+            s = jnp.where(seen, scores[p] * scale, NEG)
             e = jnp.exp(s - jnp.max(s, axis=-1, keepdims=True))
             weights.append((e * (1.0 / jnp.sum(e, axis=-1, keepdims=True))).astype(BF))
-        outs = []
+        outs = [jnp.dot(weights[p], both(vbuf, i, p), preferred_element_type=F32) for p in pairs]
         for p in pairs:
-            v2 = jnp.concatenate([vbuf[i, 2 * p], vbuf[i, 2 * p + 1]], axis=1)
-            outs.append(jnp.dot(weights[p], v2, preferred_element_type=F32))
+            o_rows[16 * p:16 * p + 8, :] = outs[p][0:8, 0:128]
+            o_rows[16 * p + 8:16 * p + 16, :] = outs[p][8:16, 128:256]
+        rows = pl.ds(pl.multiple_of(i * BLK, BLK), BLK)
+        for j in range(heads):
+            att[rows, j * 128:(j + 1) * 128] = o_rows[pl.ds(j, BLK, stride=8), :].astype(BF)
 
         @pl.when(i == HOLD)
         def _():
@@ -182,14 +167,17 @@
             for c in out_copies(i):
                 c.start()
 
-        for p in pairs:
-            o_rows[16 * p:16 * p + 8, :] = outs[p][0:8, 0:128]
-            o_rows[16 * p + 8:16 * p + 16, :] = outs[p][8:16, 128:256]
-        rows = pl.ds(pl.multiple_of(i * BLK, BLK), BLK)
-        for j in range(heads):
-            att[rows, j * 128:(j + 1) * 128] = o_rows[pl.ds(j, BLK, stride=8), :].astype(BF)
-
-    att_copy = pltpu.make_async_copy(att, att_hbm, sem.at[8])
+    for c in in_copies(0):
+        c.wait()
+    patch(kbuf, vbuf, k_rows, v_rows, pos_ref, 0)
+    score(0)
+
+    @pl.loop(0, nblk - 1)
+    def _(i):
+        step(i, True)
+
+    step(nblk - 1, False)
+    att_copy = pltpu.make_async_copy(att, att_hbm, sem.at[7])
     att_copy.start()
     att_copy.wait()
 
@@ -199,58 +187,48 @@
             c.wait()
 
 
-def attention(layer, positions, table, source, k_cache, v_cache, prev, qcols, kcols):
-    batch = positions.shape[0]
-    has_qkv = len(source) == 1
-    anyspec = pl.BlockSpec(memory_space=pl.ANY)
-    args = [positions, table, *source, k_cache, v_cache]
-    aliases = {}
-    if prev is not None:
-        aliases = {len(args): 1, len(args) + 1: 2}
-        args += list(prev)
-    cols = qcols + 2 * kcols
+def attention(layer, positions, table, hidden, norm, wq, wk, wv, k_cache, v_cache):
+    batch, dim = hidden.shape
+    qcols = wq.shape[2]
+    cols = qcols + 2 * wk.shape[2]
     nblk = batch // BLK
-    scratch = [
-        pltpu.SMEM((batch,), jnp.int32),
-        pltpu.VMEM(table.shape, F32),
-        pltpu.VMEM((cols // 256, batch, 256), BF),
-        pltpu.VMEM((batch, table.shape[1]), F32),
-        pltpu.VMEM((batch * 8, 128), F32),
-        pltpu.VMEM((batch * 8, 128), F32),
-        pltpu.VMEM((batch * 8, 128), F32),
-        pltpu.VMEM((BLK * 8, 128), F32),
-        pltpu.VMEM((batch, qcols), BF),
-        pltpu.VMEM((nblk, BLK) + k_cache.shape[2:], BF),
-        pltpu.VMEM((nblk, BLK) + v_cache.shape[2:], BF),
-        pltpu.SemaphoreType.DMA((9,)),
-        pltpu.SemaphoreType.DMA((2, nblk)),
-        pltpu.SemaphoreType.DMA((2, nblk)),
-    ]
-    if not has_qkv:
-        hidden, norm = source[:2]
-        dim = hidden.shape[1]
-        scratch += [pltpu.VMEM(hidden.shape, BF), pltpu.VMEM(norm.shape, BF), pltpu.VMEM((dim, cols), BF), pltpu.VMEM(hidden.shape, BF)]
+    hbm = pl.BlockSpec(memory_space=pltpu.HBM)
+    rows = pltpu.VMEM((batch * 8, 128), F32)
+    args = [positions, table, hidden, norm, wq, wk, wv, k_cache, v_cache]
     return pl.pallas_call(
-        functools.partial(attn_kernel, layer, has_qkv, prev is not None),
+        functools.partial(attn_kernel, layer),
         out_shape=(jax.ShapeDtypeStruct((batch, qcols), BF),
                    jax.ShapeDtypeStruct(k_cache.shape, BF), jax.ShapeDtypeStruct(v_cache.shape, BF)),
-        in_specs=[anyspec] * len(args),
-        out_specs=(anyspec, anyspec, anyspec),
-        scratch_shapes=scratch,
-        input_output_aliases=aliases,
+        in_specs=[hbm] * len(args),
+        out_specs=(hbm, hbm, hbm),
+        scratch_shapes=[
+            pltpu.SMEM((batch,), jnp.int32),
+            pltpu.VMEM(table.shape, F32),
+            pltpu.VMEM((batch, table.shape[1]), F32),
+            rows, rows, rows,
+            pltpu.VMEM((BLK * 8, 128), F32),
+            pltpu.VMEM((2, BLK // 2, 16, 256), F32),
+            pltpu.VMEM((batch, qcols), BF),
+            pltpu.VMEM((nblk, BLK) + k_cache.shape[2:], BF),
+            pltpu.VMEM((nblk, BLK) + v_cache.shape[2:], BF),
+            pltpu.VMEM(hidden.shape, BF), pltpu.VMEM(norm.shape, BF), pltpu.VMEM((dim, cols), BF), pltpu.VMEM(hidden.shape, BF),
+            pltpu.SemaphoreType.DMA((8,)),
+            pltpu.SemaphoreType.DMA((2, nblk)),
+            pltpu.SemaphoreType.DMA((2, nblk)),
+        ],
         compiler_params=pltpu.CompilerParams(vmem_limit_bytes=62 * 2**20),
-        cost_estimate=pl.CostEstimate(flops=2 * batch * 3072 * cols, bytes_accessed=76 * 2**20, transcendentals=0),
+        cost_estimate=pl.CostEstimate(flops=2 * batch * dim * cols, bytes_accessed=76 * 2**20, transcendentals=0),
         name=f"attn{layer}",
     )(*args)
 
 
-COPY_HOLD = 9
+COPY_HOLD = 11
 
 
 def write_kernel(layer, pos_hbm, new_hbm, k_hbm, v_hbm, k_prev, v_prev, ko_hbm, vo_hbm, pos_ref, new, k_rows, v_rows, kbuf, vbuf, sem, insem, outsem):
     nblk = kbuf.shape[0]
     batch = nblk * BLK
-    first = [pltpu.make_async_copy(pos_hbm, pos_ref, sem.at[0]), pltpu.make_async_copy(new_hbm, new, sem.at[1])]
+    first = [pltpu.make_async_copy(pos_hbm, pos_ref, sem.at[0]), pltpu.make_async_copy(new_hbm.at[0], new, sem.at[1])]
     for c in first:
         c.start()
 
@@ -277,22 +255,12 @@
         for r in range(4):
             k_rows[pl.ds(2 * r + h, batch, stride=8), :] = k_vec
             v_rows[pl.ds(2 * r + h, batch, stride=8), :] = v_vec
-    seq_in_group = lax.broadcasted_iota(jnp.int32, (16, 128), 0) >> 1
 
     @pl.loop(0, nblk)
     def _(i):
         for c in in_copies(i):
             c.wait()
-        for b in range(BLK):
-            pos = pos_ref[i * BLK + b]
-            group = pl.ds(pl.multiple_of((pos >> 3) * 16, 16), 16)
-            hit = seq_in_group == (pos & 7)
-            rows = pl.ds(pl.multiple_of((i * BLK + b) * 8, 8), 8)
-            for buf, rows_ref in ((kbuf, k_rows), (vbuf, v_rows)):
-                new8 = rows_ref[rows, :]
-                new16 = jnp.concatenate([new8, new8], axis=0)
-                old16 = buf[i, b, group, :].astype(F32)
-                buf[i, b, group, :] = jnp.where(hit, new16, old16).astype(BF)
+        patch(kbuf, vbuf, k_rows, v_rows, pos_ref, i)
 
         @pl.when(i == COPY_HOLD)
         def _():
@@ -315,7 +283,7 @@
 def write_rows(layer, positions, new, k_cache, v_cache, prev):
     batch = positions.shape[0]
     nblk = batch // BLK
-    anyspec = pl.BlockSpec(memory_space=pl.ANY)
+    anyspec = pl.BlockSpec(memory_space=pltpu.HBM)
     return pl.pallas_call(
         functools.partial(write_kernel, layer),
         out_shape=(jax.ShapeDtypeStruct(k_cache.shape, BF), jax.ShapeDtypeStruct(v_cache.shape, BF)),
@@ -323,7 +291,7 @@
         out_specs=(anyspec, anyspec),
         scratch_shapes=[
             pltpu.SMEM((batch,), jnp.int32),
-            pltpu.VMEM(new.shape, BF),
+            pltpu.VMEM(new.shape[1:], BF),
             pltpu.VMEM((batch * 8, 128), F32),
             pltpu.VMEM((batch * 8, 128), F32),
             pltpu.VMEM((nblk, BLK) + k_cache.shape[2:], BF),
@@ -333,7 +301,7 @@
             pltpu.SemaphoreType.DMA((2, nblk)),
         ],
         input_output_aliases={4: 0, 5: 1},
-        compiler_params=pltpu.CompilerParams(vmem_limit_bytes=67043328),
+        compiler_params=pltpu.CompilerParams(vmem_limit_bytes=50 * 2**20),
         cost_estimate=pl.CostEstimate(flops=0, bytes_accessed=67 * 2**20, transcendentals=0),
         name="write_rows",
     )(positions, new, k_cache, v_cache, *prev)
@@ -342,6 +310,7 @@
 CW = 512
 HALF = 128
 GC = 4
+SPARE = 64
 SLOT = 8
 
 
@@ -349,7 +318,7 @@
                 out_hbm, new_hbm,
                 pos_ref, table, cs, wo, wg, wu, wd, wqkv, att, x, mnorm, anorm, h, act, qkv, q_rows, k_rows, v_rows, o_rows, s_buf, new,
                 own, sd, sx, rd, rx,
-                wosem, gsem, usem, wsem, isem, sd_sem, sx_sem, sg_sem, rd_sem, rx_sem, ra_sem, osem):
+                wosem, gsem, usem, wsem, isem, hsem, sd_sem, sx_sem, sg_sem, rd_sem, rx_sem, ra_sem, osem):
     dim = x.shape[1]
     nch = dim // 2 // CW
     ncol = wg.shape[0]
@@ -383,8 +352,11 @@
     def wd_copy(layer):
         return pltpu.make_async_copy(wd_hbm.at[layer], wd, wsem.at[0])
 
-    att_copy = pltpu.make_async_copy(att_hbm, att, isem.at[0])
-    x_copy = pltpu.make_async_copy(x_hbm, x, isem.at[1])
+    def half_copy(which, half):
+        rows = pl.ds(half * HALF, HALF)
+        src, dst = ((att_hbm, att), (x_hbm, x))[which]
+        return pltpu.make_async_copy(src.at[rows], dst.at[rows], hsem.at[which, half])
+
     small = [pltpu.make_async_copy(mnorm_hbm, mnorm, isem.at[2]), pltpu.make_async_copy(anorm_hbm, anorm, isem.at[3]),
              pltpu.make_async_copy(pos_hbm, pos_ref, isem.at[4]), pltpu.make_async_copy(table_hbm, table, isem.at[5])]
     qkv_loads = [
@@ -392,13 +364,17 @@
         pltpu.make_async_copy(wk_hbm.at[1], wqkv.at[:, pl.ds(qcols, kcols)], wsem.at[2]),
         pltpu.make_async_copy(wv_hbm.at[1], wqkv.at[:, pl.ds(qcols + kcols, kcols)], wsem.at[3]),
     ]
-    att_copy.start()
+    half_copy(0, 0).start()
     wo_copy(0, 0, 0).start()
+    half_copy(1, 0).start()
+    wo_copy(0, 0, 1).start()
     wo_copy(0, 1, 0).start()
-    x_copy.start()
+    for k in range(2, nch):
+        wo_copy(0, 0, k).start()
     for k in range(1, nch):
-        wo_copy(0, 0, k).start()
         wo_copy(0, 1, k).start()
+    half_copy(0, 1).start()
+    half_copy(1, 1).start()
     for c in small:
         c.start()
 
@@ -594,8 +570,8 @@
     def att_half(half):
         return lambda: att[half * HALF:(half + 1) * HALF, :]
 
-    att_copy.wait()
-    x_copy.wait()
+    half_copy(0, 0).wait()
+    half_copy(1, 0).wait()
     reduce_start(0, att_half(0), wo, lambda side, k: wo_copy(0, side, k))()
 
     @pl.loop(0, ncol)
@@ -606,6 +582,8 @@
     wd_copy(0).start()
     for c in qkv_loads:
         c.start()
+    half_copy(0, 1).wait()
+    half_copy(1, 1).wait()
     rest = reduce_start(1, att_half(1), wo, None)
     for c in small:
         c.wait()
@@ -641,7 +619,7 @@
         qkv_rope(half)
         attend(half)
         rest = reduce_start(4 + half, att_half(half), wo, (lambda side, k: wo_copy(1, side, k)) if half == 0 else None)
-    new_copy = pltpu.make_async_copy(new, new_hbm, isem.at[6])
+    new_copy = pltpu.make_async_copy(new, new_hbm.at[0], isem.at[6])
     new_copy.start()
     for half in range(2):
         reduce_end(4 + half, rest)
@@ -669,7 +647,7 @@
     args = [positions, table, att, hidden, mnorm, anorm, wo, wg, wu, wd, wq, wk, wv, k_rows, v_rows]
     return pl.pallas_call(
         mega_kernel,
-        out_shape=(jax.ShapeDtypeStruct((batch, dim), BF), jax.ShapeDtypeStruct((4, batch, 128), BF)),
+        out_shape=(jax.ShapeDtypeStruct((batch, dim), BF), jax.ShapeDtypeStruct((SPARE, 4, batch, 128), BF)),
         in_specs=[anyspec] * len(args),
         out_specs=(anyspec, anyspec),
         scratch_shapes=[
@@ -681,7 +659,7 @@
             rows, rows, rows, rows, pltpu.VMEM((2, SLOT, 16, 256), F32), pltpu.VMEM((4, batch, 128), BF),
             pltpu.VMEM((nch, HALF, CW), F32), msg(2), msg(2), msg(4), msg(4),
             pltpu.SemaphoreType.DMA((2, nch)), pltpu.SemaphoreType.DMA((ncol,)), pltpu.SemaphoreType.DMA((ncol,)),
-            pltpu.SemaphoreType.DMA((4,)), pltpu.SemaphoreType.DMA((7,)),
+            pltpu.SemaphoreType.DMA((4,)), pltpu.SemaphoreType.DMA((7,)), pltpu.SemaphoreType.DMA((2, 2)),
             sems, sems, sems, sems, sems, sems, pltpu.SemaphoreType.DMA((2, nch)),
         ],
         compiler_params=pltpu.CompilerParams(collective_id=0, has_side_effects=True, vmem_limit_bytes=67043328),
@@ -702,8 +680,7 @@
         flat = (cache_shape[0], cache_shape[1], cache_shape[2] * cache_shape[3], cache_shape[4])
         k_flat, v_flat = k_cache.reshape(flat), v_cache.reshape(flat)
         table = jnp.asarray(rope_table(cache_shape[2], cache_shape[4]))
-        source = (hidden, attn_norm, w_query, w_key, w_value)
-        att, *caches = attention(0, positions, table, source, k_flat, v_flat, None, w_query.shape[2], w_key.shape[2])
+        att, *caches = attention(0, positions, table, hidden, attn_norm, w_query, w_key, w_value, k_flat, v_flat)
         rows = (cache_shape[0], -1, cache_shape[4])
         hidden, new = mega(positions, table, att, hidden, mlp_norm, attn_norm, w_out, w_gate, w_up, w_down, w_query, w_key, w_value,
                            k_cache.reshape(rows), v_cache.reshape(rows))

time: 131 us -> 131 us (level)
    unnamed x1 -> x5, local copies, waits for them, and re-layouts: 2.65 us -> 1.82 us
where the time goes in v5:
time: 131 us
  Pallas kernels  128 us (98%)
  local copies, waits for them, and re-layouts  1.82 us (1%)
    pallas_call x1, Pallas kernels, mega(): pl.pallas_call(mega_kernel, out_shape=(jax.ShapeDtypeStruct((batch, dim),...  83.3 us
    pallas_call x1, Pallas kernels, attention(): pl.pallas_call(functools.partial(attn_kernel, layer), out_shape=(jax.Shap...  23.6 us
    pallas_call x1, Pallas kernels, write_rows(): pl.pallas_call(functools.partial(write_kernel, layer), out_shape=(jax.Sha...  21.3 us

profile of v5, /device:TPU:0, one launch (start us, length us, event | category | flops | bytes accessed | tf_op | source)
XLA Modules:
  0.0 130.7 jit_solution(7000487212980337035)
XLA Ops:
  0.6 23.6 %attn0.1 = (bf16[256,768]{1,0:T(8,128)(2,1)}, bf16[2,256,256,128]{3,2,1,0:T(8,128)(2,1)}, bf16[2,256,256,128]{3,2,1,0:T(8,128)(2,1)}) custom-call(s32[256]{0:T(256)} %pos_hbm.5, f32[128,256]{1,0:T(8,128)} %constant.2.clone.table_hbm, bf16[256,3072]{1,0:T(8,128)(2,1)} %x_hbm.3, bf16[2,3072]{1,0:T(2,128)(2,1)} %anorm_hbm.1, bf16[2,3072,768]{2,1,0:T(8,128)(2,1)} %wq_hbm.3, ...), custom_call_target="tpu_custom_call" | custom-call | flops 2013265920 | bytes 79691776 | tf_op jit(solution)/shard_map/attn0/pallas_call | solution.py:198
  24.2 83.3 %mega.1 = (bf16[256,3072]{1,0:T(8,128)(2,1)}, bf16[64,4,256,128]{3,2,1,0:T(8,128)(2,1)}) custom-call(s32[256]{0:T(256)} %pos_hbm.5, f32[128,256]{1,0:T(8,128)} %constant.2.clone.table_hbm, bf16[256,768]{1,0:T(8,128)(2,1)} %get-tuple-element.10.att_hbm, bf16[256,3072]{1,0:T(8,128)(2,1)} %x_hbm.3, bf16[2,3072]{1,0:T(2,128)(2,1)} %mnorm_hbm.1, ...), custom_call_target="tpu_custom_call" | custom-call | tf_op jit(solution)/shard_map/mega/pallas_call | solution.py:648
  107.5 0.0 copy-start
  107.5 0.7 copy-done
  108.2 0.0 copy-start.1
  108.2 21.3 %write_rows.1 = (bf16[2,256,256,128]{3,2,1,0:T(8,128)(2,1)}, bf16[2,256,256,128]{3,2,1,0:T(8,128)(2,1)}) custom-call(s32[256]{0:T(256)S(1)} %copy-done, bf16[64,4,256,128]{3,2,1,0:T(8,128)(2,1)} %get-tuple-element.12.new_hbm, bf16[2,256,256,128]{3,2,1,0:T(8,128)(2,1)} %bitcast.8, ...), custom_call_target="tpu_custom_call", output_to_operand_aliasing={{0}: (4, {}), {1}: (5, {})} | custom-call | bytes 70254592 | tf_op jit(solution)/shard_map/write_rows/pallas_call | solution.py:287
  129.6 0.0 copy-done.1
  129.6 1.1 copy.22
Async XLA Ops:
  107.5 0.7 copy-start
  108.2 21.4 %copy-start.1 = (bf16[256,3072]{1,0:T(8,128)(2,1)S(1)}, bf16[256,3072]{1,0:T(8,128)(2,1)}, u32[]{:S(2)}) copy-start(bf16[256,3072]{1,0:T(8,128)(2,1)} %get-tuple-element.20) | copy-start | bytes 4718596

commit v6 on v5

--- a/solution.py
+++ b/solution.py
@@ -33,6 +33,7 @@
 
 
 BLK = 16
+ROOM = 1 << 23
 HOLD = 6
 
 
@@ -50,7 +51,7 @@
             buf[i, b, group, :] = jnp.where(hit, new16, old16).astype(BF)
 
 
-def attn_kernel(layer, pos_hbm, table_hbm, x_hbm, norm_hbm, wq_hbm, wk_hbm, wv_hbm, k_hbm, v_hbm, att_hbm, ko_hbm, vo_hbm,
+def attn_kernel(layer, pos_hbm, table_hbm, x_hbm, norm_hbm, wq_hbm, wk_hbm, wv_hbm, k_hbm, v_hbm, att_hbm, ko_hbm, vo_hbm, where_hbm,
                 pos_ref, table, cs, q_rows, k_rows, v_rows, o_rows, s_buf, att, kbuf, vbuf, x_buf, norm, w_buf, h_buf, sem, insem, outsem):
     nblk = kbuf.shape[0]
     batch = nblk * BLK
@@ -177,9 +178,11 @@
         step(i, True)
 
     step(nblk - 1, False)
-    att_copy = pltpu.make_async_copy(att, att_hbm, sem.at[7])
-    att_copy.start()
-    att_copy.wait()
+    results = [pltpu.make_async_copy(att, att_hbm, sem.at[7]), pltpu.make_async_copy(pos_ref, where_hbm.at[pl.ds(0, batch)], sem.at[8])]
+    for c in results:
+        c.start()
+    for c in results:
+        c.wait()
 
     @pl.loop(0, nblk)
     def _(i):
@@ -198,9 +201,10 @@
     return pl.pallas_call(
         functools.partial(attn_kernel, layer),
         out_shape=(jax.ShapeDtypeStruct((batch, qcols), BF),
-                   jax.ShapeDtypeStruct(k_cache.shape, BF), jax.ShapeDtypeStruct(v_cache.shape, BF)),
+                   jax.ShapeDtypeStruct(k_cache.shape, BF), jax.ShapeDtypeStruct(v_cache.shape, BF),
+                   jax.ShapeDtypeStruct((ROOM,), jnp.int32)),
         in_specs=[hbm] * len(args),
-        out_specs=(hbm, hbm, hbm),
+        out_specs=(hbm, hbm, hbm, hbm),
         scratch_shapes=[
             pltpu.SMEM((batch,), jnp.int32),
             pltpu.VMEM(table.shape, F32),
@@ -212,7 +216,7 @@
             pltpu.VMEM((nblk, BLK) + k_cache.shape[2:], BF),
             pltpu.VMEM((nblk, BLK) + v_cache.shape[2:], BF),
             pltpu.VMEM(hidden.shape, BF), pltpu.VMEM(norm.shape, BF), pltpu.VMEM((dim, cols), BF), pltpu.VMEM(hidden.shape, BF),
-            pltpu.SemaphoreType.DMA((8,)),
+            pltpu.SemaphoreType.DMA((9,)),
             pltpu.SemaphoreType.DMA((2, nblk)),
             pltpu.SemaphoreType.DMA((2, nblk)),
         ],
@@ -228,7 +232,7 @@
 def write_kernel(layer, pos_hbm, new_hbm, k_hbm, v_hbm, k_prev, v_prev, ko_hbm, vo_hbm, pos_ref, new, k_rows, v_rows, kbuf, vbuf, sem, insem, outsem):
     nblk = kbuf.shape[0]
     batch = nblk * BLK
-    first = [pltpu.make_async_copy(pos_hbm, pos_ref, sem.at[0]), pltpu.make_async_copy(new_hbm.at[0], new, sem.at[1])]
+    first = [pltpu.make_async_copy(pos_hbm.at[pl.ds(0, batch)], pos_ref, sem.at[0]), pltpu.make_async_copy(new_hbm.at[0], new, sem.at[1])]
     for c in first:
         c.start()
 
@@ -281,7 +285,7 @@
 
 
 def write_rows(layer, positions, new, k_cache, v_cache, prev):
-    batch = positions.shape[0]
+    batch = k_cache.shape[1]
     nblk = batch // BLK
     anyspec = pl.BlockSpec(memory_space=pltpu.HBM)
     return pl.pallas_call(
@@ -309,7 +313,7 @@
 
 CW = 512
 HALF = 128
-GC = 4
+GC = 8
 SPARE = 64
 SLOT = 8
 
@@ -680,11 +684,11 @@
         flat = (cache_shape[0], cache_shape[1], cache_shape[2] * cache_shape[3], cache_shape[4])
         k_flat, v_flat = k_cache.reshape(flat), v_cache.reshape(flat)
         table = jnp.asarray(rope_table(cache_shape[2], cache_shape[4]))
-        att, *caches = attention(0, positions, table, hidden, attn_norm, w_query, w_key, w_value, k_flat, v_flat)
+        att, *caches, where = attention(0, positions, table, hidden, attn_norm, w_query, w_key, w_value, k_flat, v_flat)
         rows = (cache_shape[0], -1, cache_shape[4])
         hidden, new = mega(positions, table, att, hidden, mlp_norm, attn_norm, w_out, w_gate, w_up, w_down, w_query, w_key, w_value,
                            k_cache.reshape(rows), v_cache.reshape(rows))
-        caches = write_rows(1, positions, new, k_flat, v_flat, caches)
+        caches = write_rows(1, where, new, k_flat, v_flat, caches)
         return hidden, caches[0].reshape(cache_shape), caches[1].reshape(cache_shape)
 
     return jax.shard_map(local_step, mesh=mesh, in_specs=(row_spec, pos_spec, cache_spec, cache_spec, norm_spec, col_spec, col_spec, col_spec, split_rows, norm_spec, col_spec, col_spec, split_rows), out_specs=(row_spec, cache_spec, cache_spec), check_vma=False)

time: 131 us -> 130 us (level)
  no operation moved by 1% of the time
where the time goes in v6:
time: 130 us
  Pallas kernels  128 us (98%)
    pallas_call x1, Pallas kernels, mega(): pl.pallas_call(mega_kernel, out_shape=(jax.ShapeDtypeStruct((batch, dim),...  83 us
    pallas_call x1, Pallas kernels, attention(): pl.pallas_call(functools.partial(attn_kernel, layer), out_shape=(jax.Shap...  23.6 us
    pallas_call x1, Pallas kernels, write_rows(): pl.pallas_call(functools.partial(write_kernel, layer), out_shape=(jax.Sha...  21.3 us

profile of v6, /device:TPU:0, one launch (start us, length us, event | category | flops | bytes accessed | tf_op | source)
XLA Modules:
  0.0 129.7 jit_solution(6937757639052574371)
XLA Ops:
  0.6 23.6 %attn0.1 = (bf16[256,768]{1,0:T(8,128)(2,1)}, bf16[2,256,256,128]{3,2,1,0:T(8,128)(2,1)}, bf16[2,256,256,128]{3,2,1,0:T(8,128)(2,1)}, s32[8388608]{0:T(1024)}) custom-call(s32[256]{0:T(256)} %pos_hbm.3, f32[128,256]{1,0:T(8,128)} %constant.2.clone.table_hbm, bf16[256,3072]{1,0:T(8,128)(2,1)} %x_hbm.3, bf16[2,3072]{1,0:T(2,128)(2,1)} %anorm_hbm.1, ...), custom_call_target="tpu_custom_call" | custom-call | flops 2013265920 | bytes 79691776 | tf_op jit(solution)/shard_map/attn0/pallas_call | solution.py:201
  24.2 83.0 %mega.1 = (bf16[256,3072]{1,0:T(8,128)(2,1)}, bf16[64,4,256,128]{3,2,1,0:T(8,128)(2,1)}) custom-call(s32[256]{0:T(256)} %pos_hbm.3, f32[128,256]{1,0:T(8,128)} %constant.2.clone.table_hbm, bf16[256,768]{1,0:T(8,128)(2,1)} %get-tuple-element.11.att_hbm, bf16[256,3072]{1,0:T(8,128)(2,1)} %x_hbm.3, bf16[2,3072]{1,0:T(2,128)(2,1)} %mnorm_hbm.1, ...), custom_call_target="tpu_custom_call" | custom-call | tf_op jit(solution)/shard_map/mega/pallas_call | solution.py:652
  107.2 0.0 copy-start
  107.2 21.3 %write_rows.1 = (bf16[2,256,256,128]{3,2,1,0:T(8,128)(2,1)}, bf16[2,256,256,128]{3,2,1,0:T(8,128)(2,1)}) custom-call(s32[8388608]{0:T(1024)} %get-tuple-element.13.pos_hbm, bf16[64,4,256,128]{3,2,1,0:T(8,128)(2,1)} %get-tuple-element.14.new_hbm, bf16[2,256,256,128]{3,2,1,0:T(8,128)(2,1)} %bitcast.8, ...), custom_call_target="tpu_custom_call", output_to_operand_aliasing={{0}: (4, {}), {1}: (5, {})} | custom-call | bytes 70254592 | tf_op jit(solution)/shard_map/write_rows/pallas_call | solution.py:291
  128.5 0.0 copy-done
  128.6 1.1 copy.22
Async XLA Ops:
  107.2 21.3 %copy-start = (bf16[256,3072]{1,0:T(8,128)(2,1)S(1)}, bf16[256,3072]{1,0:T(8,128)(2,1)}, u32[]{:S(2)}) copy-start(bf16[256,3072]{1,0:T(8,128)(2,1)} %get-tuple-element.22) | copy-start | bytes 4718596
